TPU v7x, 128 devices: a whole 4x4x4 slice. The times are simulated.
128 devices in a mesh: dom: 128 (over y, z, x, core).
Axes of the slice: x: 4, y: 4, z: 4, core: 2. Of those that a mesh axis runs over, the one named last changes fastest.
Arguments:
- right_side: float32 [131072, 3], P('dom'), may hold values from -10 to 10
- fine_diagonal: float32 [131072, 3], P('dom'), may hold values from 2 to 4
- fine_columns: int32 [131072, 27], P('dom'), may hold values from 0 to 131071, as said below
- fine_blocks: float32 [131072, 27, 3, 3], P('dom'), may hold values from -0.625 to 0.625
- aggregate_of_node: int32 [131072], P('dom'), may hold values from 0 to 31, as said below
- coarse_row_of_aggregate: int32 [4096], P('dom'), may hold values from 0 to 4095, as said below
- coarse_diagonal: float32 [4096, 3], P('dom'), may hold values from 2 to 4
- coarse_columns: int32 [4096, 27], P('dom'), may hold values from 0 to 4095
- coarse_blocks: float32 [4096, 27, 3, 3], P('dom'), may hold values from -0.625 to 0.625
Outputs:
- solution: float32 [131072, 3], P('dom')
- correction: float32 [4096, 3], P('dom')
Inputs may be any that keep to these rules, and one draw needn't show every extreme that they name: Every entry of fine_columns differs from its row number by at most 256, and some entry by exactly 256. `aggregate_of_node`: on each device every aggregate number 0 to 31 is used by at least one of its nodes. coarse_row_of_aggregate is a permutation of 0 to 4095; among the 32 aggregates of one device (an aligned block of entries) at most 8 get rows of any one owner, and exactly 8 for some owner.
All inputs are finite; a program needn't handle non-finite values.
Results may differ from a plain program's by a relative error of at most 0.0003.
Values sent between devices are 32-bit elements.
No kernel may reach another device: no remote copies, remote signals or barrier semaphores. Data moves between devices by JAX's collectives and lax.ppermute only.
A program may use at most 64 MiB of HBM per device.

v0:
```python
import jax
import jax.numpy as jnp
from jax import lax
from jax.experimental import pallas as pl
from jax.experimental.pallas import tpu as pltpu
from jax.sharding import PartitionSpec as P


DOM = "dom"
PEERS = 32
NEAR = 8
PARTS = PEERS // NEAR
PIECES = 128 // PEERS
UNROLL = 8
CSWEEPS = 6
damping = 0.7
highest = lax.Precision.HIGHEST

ROWS = 1024
LANES = 128
SLOTS = 27
FULL = 24
HALO = 256
WIDE = 512
BLOCKS = ROWS // LANES
P_COL = 9 * FULL
P_BTAIL = P_COL + FULL
P_CTAIL = P_BTAIL + 27
P_RHS = P_CTAIL + 3
P_DIA = P_RHS + 6
P_ROW = P_DIA + 6
P_ALL = 288
f32 = jnp.float32
i32 = jnp.int32


def lanes(start, size=LANES):
    if isinstance(start, int):
        return slice(start, start + size)
    return pl.ds(pl.multiple_of(start, LANES), size)


def picked(row, where):
    return jnp.take_along_axis(
        jnp.broadcast_to(row, where.shape), where, axis=1, mode="promise_in_bounds"
    )


def pack_kernel(rhs_in, dia_in, col_in, blk_in, agg_in, owner_in, ccol_in, cblk_in,
                up, down, node_row, send, rhs, dia, col, blk, agg, owner, ccol, cblk, sem):
    copies = [(ccol_in, ccol), (cblk_in, cblk)]
    copies += [(rhs_in, rhs), (dia_in, dia), (agg_in, agg), (owner_in, owner)]
    for t, near in enumerate((ROWS - HALO, 0)):
        copies.append((col_in.at[:, lanes(near, HALO)], col.at[t]))
        copies.append((blk_in.at[:, :, :, lanes(near, HALO)], blk.at[t]))
    copies = [pltpu.make_async_copy(a, b, sem.at[n]) for n, (a, b) in enumerate(copies)]
    for c in copies:
        c.start()
    for c in copies[:2]:
        c.wait()
    pack_coarse(ccol, cblk, send)
    for c in copies[2:]:
        c.wait()
    table = jnp.concatenate([owner[...]] * 4, axis=1)
    found = picked(table, agg[...]).astype(f32)
    node_row[...] = found
    for t, (out, wide) in enumerate(((up, ROWS - WIDE), (down, 0))):
        for i in range(3):
            for j in range(3):
                g = 3 * i + j
                out[g * FULL : (g + 1) * FULL, :] = blk[t, i, j, 0:FULL, :]
                out[P_BTAIL + 3 * g : P_BTAIL + 3 * g + 3, :] = blk[t, i, j, FULL:SLOTS, :]
        out[P_COL : P_COL + FULL, :] = col[t, 0:FULL, :].astype(f32)
        out[P_CTAIL : P_CTAIL + 3, :] = col[t, FULL:SLOTS, :].astype(f32)
        for h in range(2):
            out[P_RHS + 3 * h : P_RHS + 3 * h + 3, :] = rhs[:, lanes(wide + HALO * h, HALO)]
            out[P_DIA + 3 * h : P_DIA + 3 * h + 3, :] = dia[:, lanes(wide + HALO * h, HALO)]
            for q in range(2):
                s = wide // LANES + 2 * h + q
                out[P_ROW + h : P_ROW + h + 1, lanes(LANES * q)] = found[s : s + 1, :]
        out[P_ROW + 2 : P_ALL, :] = jnp.zeros((P_ALL - P_ROW - 2, HALO), f32)


def pulled_block(columns, blocks, table, first_chunk):
    total = [None, None, None]
    for part in range(4):
        where = columns(part)
        chunk = lax.shift_right_arithmetic(where, 7)
        lane = lax.bitwise_and(where, 127)
        near = [jnp.zeros(where.shape, f32) for _ in range(3)]
        for c in range(5):
            here = chunk == c
            for j in range(3):
                row = table[j : j + 1, lanes(first_chunk * LANES + c * LANES)]
                near[j] = jnp.where(here, picked(row, lane), near[j])
        for i in range(3):
            s = blocks(i, 0, part) * near[0]
            s = s + blocks(i, 1, part) * near[1]
            s = s + blocks(i, 2, part) * near[2]
            if part < 3:
                total[i] = s if total[i] is None else total[i] + s
            else:
                total[i] = jnp.sum(total[i], axis=0, keepdims=True) + jnp.sum(
                    s, axis=0, keepdims=True
                )
    return total


def local_getters(col, blk, start, b):
    def columns(part):
        lo, hi = 8 * part, min(8 * part + 8, SLOTS)
        return col[lo:hi, lanes(b * LANES)] - start

    def blocks(i, j, part):
        lo, hi = 8 * part, min(8 * part + 8, SLOTS)
        return blk[i, j, lo:hi, lanes(b * LANES)]

    return columns, blocks


def halo_getters(halo, start, b):
    def columns(part):
        if part < 3:
            got = halo[P_COL + 8 * part : P_COL + 8 * part + 8, lanes(b * LANES)]
        else:
            got = halo[P_CTAIL : P_CTAIL + 3, lanes(b * LANES)]
        return got.astype(i32) - start

    def blocks(i, j, part):
        g = 3 * i + j
        if part < 3:
            return halo[g * FULL + 8 * part : g * FULL + 8 * part + 8, lanes(b * LANES)]
        return halo[P_BTAIL + 3 * g : P_BTAIL + 3 * g + 3, lanes(b * LANES)]

    return columns, blocks


def wide_vector(out, local, before, after, row):
    out[:, lanes(WIDE, ROWS)] = local[...]
    for h in range(2):
        out[:, lanes(HALO * h, HALO)] = before[row + 3 * h : row + 3 * h + 3, :]
        out[:, lanes(WIDE + ROWS + HALO * h, HALO)] = after[row + 3 * h : row + 3 * h + 3, :]


def smoothed(table, pulled, rhs, dia, at):
    pull = jnp.concatenate(pulled, axis=0)
    s = table[:, lanes(at)]
    b = rhs[:, lanes(at)]
    d = dia[:, lanes(at)]
    return s + damping * (b - (d * s - pull)) / d


def sweep_halo(out, table, rhs, dia, halo, base, first):
    for b in range(2):
        at = first + LANES * b
        start = base + (at - WIDE) - 2 * LANES
        cols, blks = halo_getters(halo, start, b)
        pull = pulled_block(cols, blks, table, at // LANES - 2)
        out[:, lanes(at)] = smoothed(table, pull, rhs, dia, at)


def each_block(step):
    def some(t, carry):
        for u in range(UNROLL):
            step(t * UNROLL + u)
        return carry

    lax.fori_loop(0, BLOCKS // UNROLL, some, 0)


def own_block(table, col, blk, base, b):
    start = base + b * LANES - 2 * LANES
    cols, blks = local_getters(col, blk, start, b)
    return pulled_block(cols, blks, table, b + WIDE // LANES - 2)


def pre_kernel(base_ref, rhs, dia, col, blk, agg, owner_row, cdia, before, after,
               send, first_iter, keep_rhs, keep_dia, up2, down2, one, two, res):
    base = base_ref[0]
    wide_vector(keep_rhs, rhs, before, after, P_RHS)
    wide_vector(keep_dia, dia, before, after, P_DIA)
    raw = keep_dia[...]
    keep_dia[...] = jnp.where(raw == 0.0, 1.0, raw)
    one[...] = damping * keep_rhs[...] / keep_dia[...]
    two[...] = jnp.zeros(two.shape, f32)
    sweep_halo(two, one, keep_rhs, keep_dia, before, base, WIDE - HALO)
    sweep_halo(two, one, keep_rhs, keep_dia, after, base, WIDE + ROWS)

    def second(b):
        at = WIDE + b * LANES
        pull = own_block(one, col, blk, base, b)
        two[:, lanes(at)] = smoothed(one, pull, keep_rhs, keep_dia, at)

    each_block(second)

    def third(b):
        at = WIDE + b * LANES
        pull = jnp.concatenate(own_block(two, col, blk, base, b), axis=0)
        s, d = two[:, lanes(at)], keep_dia[:, lanes(at)]
        res[0:3, lanes(b * LANES)] = keep_rhs[:, lanes(at)] - (d * s - pull)

    res[...] = jnp.zeros(res.shape, f32)
    each_block(third)
    first_iter[...] = two[...]
    up2[...] = two[:, lanes(WIDE + ROWS - WIDE, HALO)]
    down2[...] = two[:, lanes(WIDE + HALO, HALO)]
    label = lax.broadcasted_iota(i32, (32, LANES), 0)
    sums = None
    for b in range(BLOCKS):
        member = (label == jnp.broadcast_to(agg[b : b + 1, :], (32, LANES))).astype(f32)
        part = lax.dot_general(
            res[:, lanes(b * LANES)], member, (((1,), (1,)), ((), ())),
            precision=highest, preferred_element_type=f32,
        )
        sums = part if sums is None else sums + part
    row = jnp.concatenate(
        [sums[0:1], sums[1:2], sums[2:3], owner_row[...].astype(f32)], axis=1
    )
    send[:, 0, :] = jnp.broadcast_to(row, (LANES, LANES))
    row = jnp.concatenate(
        [cdia[0:1], cdia[1:2], cdia[2:3], jnp.ones((1, 32), f32)], axis=1
    )
    send[:, 1, :] = jnp.broadcast_to(row, (LANES, LANES))


def bit_of(p, at):
    return lax.bitwise_and(lax.shift_right_logical(p, at), 1)


def bit_parity(p, at):
    return lax.bitwise_xor(bit_of(p, at), bit_of(p, at + 1))


def lane_of_device(p, me):
    off = lax.bitwise_xor(p, me)
    rest = 4 * bit_of(p, 6) + 2 * bit_of(p, 4) + bit_of(p, 2)
    return (
        64 * bit_parity(off, 1) + 32 * bit_of(off, 0) + 16 * bit_parity(off, 5) + 8 * bit_parity(off, 3)
        + rest
    )


def device_of_lane(q, me):
    def last(relative, at, first):
        return lax.bitwise_xor(lax.bitwise_xor(relative, bit_parity(me, at)), first)

    x, z, y = bit_of(q, 0), bit_of(q, 1), bit_of(q, 2)
    p = 64 * y + 32 * last(bit_of(q, 4), 5, y) + 16 * z + 8 * last(bit_of(q, 3), 3, z)
    core = lax.bitwise_xor(bit_of(q, 5), bit_of(me, 0))
    return p + 4 * x + 2 * last(bit_of(q, 6), 1, x) + core


def row_groups():
    def member(kind, m):
        y, z, x = m >> 2, m >> 1 & 1, m & 1
        py, pz, px, core = kind >> 3, kind >> 2 & 1, kind >> 1 & 1, kind & 1
        return 64 * y + 32 * (y ^ py) + 16 * z + 8 * (z ^ pz) + 4 * x + 2 * (x ^ px) + core

    return [[member(kind, m) for m in range(NEAR)] for kind in range(16)]


def pack_coarse(col, blk, send):
    def turned(a):
        z = jnp.transpose(jnp.concatenate([a, jnp.zeros((32, 5), f32)], axis=1))
        return jnp.concatenate([z] * 4, axis=1)

    columns = turned(col[...].astype(f32))
    kind = lax.bitwise_and(columns.astype(i32), 7)
    tile = (8, LANES)
    sub = lax.broadcasted_iota(i32, tile, 0)
    count = jnp.zeros(tile, i32)
    match, earlier = [], []
    for k in range(SLOTS):
        here = sub == jnp.broadcast_to(kind[k : k + 1], tile)
        match.append(here)
        earlier.append(count)
        count = count + here.astype(i32)
    left = jnp.zeros((1, LANES), i32)
    start = []
    for n in range(16):
        if n >= 8:
            start.append(left)
        left = jnp.maximum(left + count[n % 8 : n % 8 + 1] - 4, 0)
    start = jnp.concatenate(start, axis=0) + 4 * sub
    place = 4 * sub + lax.shift_right_logical(lax.broadcasted_iota(i32, tile, 1), 5)
    slot = jnp.full(tile, 31, i32)
    for k in range(SLOTS):
        at = jnp.sum(jnp.where(match[k], start + earlier[k], 0), axis=0, keepdims=True)
        slot = jnp.where(place == jnp.broadcast_to(lax.bitwise_and(at, 31), tile), k, slot)
    inner, outer = lax.bitwise_and(slot, 7), lax.shift_right_logical(slot, 3)

    def placed(z):
        got = None
        for g in range(4):
            part = jnp.take_along_axis(
                z[8 * g : 8 * g + 8], inner, axis=0, mode="promise_in_bounds"
            )
            got = part if got is None else jnp.where(outer == g, part, got)
        return got

    parts = [placed(turned(blk[i, j])) for i in range(3) for j in range(3)]
    parts.append(jnp.where(slot == 31, sub.astype(f32), placed(columns)))
    for m in range(10):
        for d in range(NEAR):
            send[d, 8 * m : 8 * m + 8, :] = parts[m]


def spread(parts):
    group = lax.shift_right_logical(lax.broadcasted_iota(i32, parts[0].shape, 1), 5)
    return jnp.where(group == 0, parts[0], jnp.where(group == 1, parts[1], parts[2]))


def coarse_lookup(table, chunk, lane):
    near = [jnp.zeros(chunk.shape, f32) for _ in range(3)]
    for c in range(32):
        here = chunk == c
        for j in range(3):
            row = table[32 * j + c : 32 * j + c + 1, :]
            near[j] = jnp.where(here, picked(row, lane), near[j])
    return near


def coarse_step(table, where, passes, data, own, rhs, dia, gather):
    gather[...] = jnp.zeros(gather.shape, f32)

    def one_pass(t, carry):
        rows = [
            [pltpu.roll(table[32 * j + 8 * v : 32 * j + 8 * v + 8, :], t, axis=0) for v in range(4)]
            for j in range(3)
        ]
        for d in range(PEERS):
            w = where[d]
            code, lane = lax.bitwise_and(w, 31), lax.shift_right_logical(w, 5)
            near = [jnp.zeros((8, LANES), f32) for _ in range(3)]
            for v in range(4):
                here = code == 4 * t + v
                for j in range(3):
                    near[j] = jnp.where(here, picked(rows[j][v], lane), near[j])
            for i in range(3):
                a = data[d // NEAR][d % NEAR, lanes8(3 * i), :] * near[0]
                a = a + data[d // NEAR][d % NEAR, lanes8(3 * i + 1), :] * near[1]
                a = a + data[d // NEAR][d % NEAR, lanes8(3 * i + 2), :] * near[2]
                gather[i, d : d + 1, :] += jnp.sum(a, axis=0, keepdims=True)
        return carry

    lax.fori_loop(0, passes, one_pass, 0)
    parts = []
    for i in range(3):
        s = gather[i]
        s = s + pltpu.roll(s, 64, axis=1)
        parts.append(s + pltpu.roll(s, 32, axis=1))
    return own + damping * (rhs - (dia * own - spread(parts))) / dia


def lanes8(m):
    return slice(8 * m, 8 * m + 8)


def coarse_first_kernel(base_ref, sums, *rest):
    data = rest[:PARTS]
    new, rhs, dia, where, passes, table, gather, left, right = rest[PARTS:]
    me = lax.shift_right_logical(base_ref[0], 10)
    got = jnp.transpose(sums[:, 0, :])
    rows = got[96:128].astype(i32)
    s = got[0:96]
    split = []
    for _ in range(3):
        t = s.astype(jnp.bfloat16).astype(f32)
        split.append(t)
        s = s - t
    chunk = lax.broadcasted_iota(i32, (32, LANES), 0)
    place = lax.broadcasted_iota(i32, (LANES, LANES), 0)
    low = lax.bitwise_and(rows, 31)
    lane = lane_of_device(lax.shift_right_logical(rows, 5), me)
    for a in range(32):
        here = chunk == jnp.broadcast_to(low[a : a + 1], (32, LANES))
        for t in range(3):
            for i in range(3):
                value = jnp.broadcast_to(split[t][32 * i + a : 32 * i + a + 1], (32, LANES))
                left[96 * t + 32 * i : 96 * t + 32 * i + 32, lanes(LANES * a)] = jnp.where(
                    here, value, 0.0
                ).astype(jnp.bfloat16)
        right[:, lanes(LANES * a)] = jnp.where(
            place == jnp.broadcast_to(lane[a : a + 1], (LANES, LANES)), 1.0, 0.0
        ).astype(jnp.bfloat16)
    both = lax.dot_general(
        left[...], right[...], (((1,), (1,)), ((), ())), preferred_element_type=f32
    )
    crhs = both[0:96] + both[96:192] + both[192:288]
    order = device_of_lane(lax.broadcasted_iota(i32, (96, LANES), 1), me)
    cdia = jnp.take_along_axis(
        jnp.transpose(sums[:, 1, :])[0:96], order, axis=1, mode="promise_in_bounds"
    )
    pad = jnp.zeros((32, LANES), f32)
    first = jnp.concatenate([damping * crhs / cdia, pad], axis=0)
    table[...] = first
    own = jnp.transpose(first)[0:PEERS]
    rhs[...] = jnp.transpose(jnp.concatenate([crhs, pad], axis=0))[0:PEERS]
    dia[...] = jnp.transpose(jnp.concatenate([cdia, pad + 1.0], axis=0))[0:PEERS]
    sub = lax.broadcasted_iota(i32, (8, LANES), 0)
    most = jnp.zeros((8, LANES), i32)
    for d in range(PEERS):
        c = data[d // NEAR][d % NEAR, 72:80, :].astype(i32)
        off = lax.bitwise_and(sub - c, 7)
        most = jnp.maximum(most, off)
        at = lane_of_device(lax.shift_right_logical(c, 5), me)
        code = lax.bitwise_and(lax.shift_right_logical(c, 3), 3) + lax.shift_left(off, 2)
        where[d] = code + lax.shift_left(at, 5)
    most = jnp.max(most.astype(f32)).astype(i32) + 1
    passes[...] = jnp.broadcast_to(most, passes.shape)
    new[...] = coarse_step(
        table, where, most, data, own, rhs[...], dia[...], gather
    )


def gathered(table, pieces, mine):
    row = 0
    for piece in pieces:
        size = piece.shape[0]
        mine[row : row + size, :] = piece[...]
        row += size
    table[...] = jnp.transpose(mine[...])


def coarse_kernel(base_ref, passes, *rest):
    pieces, (rhs, dia, where) = rest[:PIECES], rest[PIECES : PIECES + 3]
    data = rest[PIECES + 3 : PIECES + 3 + PARTS]
    new, table, mine, gather = rest[PIECES + 3 + PARTS :]
    gathered(table, pieces, mine)
    new[...] = coarse_step(
        table, where, passes[...][0, 0], data, pieces[0][...], rhs[...], dia[...], gather
    )


def post_kernel(base_ref, *rest):
    pieces = rest[:PIECES]
    (first_iter, rhs, dia, col, blk, node_row, before, after, before2, after2,
     out, correction, table, mine, one, two) = rest[PIECES:]
    base = base_ref[0]
    me = lax.shift_right_logical(base, 10)
    gathered(table, pieces, mine)
    row = mine[pl.ds(lane_of_device(me, me), 1), :]
    correction[...] = jnp.concatenate([row[:, 32 * i : 32 * i + 32] for i in range(3)], axis=0)
    one[...] = first_iter[...]
    one[:, lanes(0, HALO)] = before2[...]
    one[:, lanes(WIDE + ROWS + HALO, HALO)] = after2[...]
    edge = [
        h[P_ROW + t : P_ROW + t + 1, lanes(LANES * q)]
        for h in (before, after) for t in range(2) for q in range(2)
    ]
    edge = jnp.concatenate(edge, axis=0)

    def found(rows):
        rows = rows.astype(i32)
        lane = lane_of_device(lax.shift_right_logical(rows, 5), me)
        return coarse_lookup(table, lax.bitwise_and(rows, 31), lane)

    own, far = found(node_row[...]), found(edge)
    for s in range(16):
        if s < 4:
            row = [f[s : s + 1, :] for f in far]
        elif s < 12:
            row = [f[s - 4 : s - 3, :] for f in own]
        else:
            row = [f[s - 8 : s - 7, :] for f in far]
        one[:, lanes(s * LANES)] = one[:, lanes(s * LANES)] + jnp.concatenate(row, axis=0)
    two[...] = jnp.zeros(two.shape, f32)
    sweep_halo(two, one, rhs, dia, before, base, WIDE - HALO)
    sweep_halo(two, one, rhs, dia, after, base, WIDE + ROWS)

    def first(b):
        at = WIDE + b * LANES
        pull = own_block(one, col, blk, base, b)
        two[:, lanes(at)] = smoothed(one, pull, rhs, dia, at)

    def second(b):
        at = WIDE + b * LANES
        pull = own_block(two, col, blk, base, b)
        out[:, lanes(b * LANES)] = smoothed(two, pull, rhs, dia, at)

    each_block(first)
    each_block(second)


def call(kernel, outs, args, scratch=(), scalars=0, limit=12):
    vmem = pl.BlockSpec(memory_space=pltpu.VMEM)
    smem = pl.BlockSpec(memory_space=pltpu.SMEM)
    return pl.pallas_call(
        kernel,
        in_specs=[smem] * scalars + [vmem] * (len(args) - scalars),
        out_specs=[vmem] * len(outs),
        out_shape=[jax.ShapeDtypeStruct(o, t) for o, t in outs],
        scratch_shapes=[
            pltpu.VMEM(*s) if isinstance(s[0], tuple) else pltpu.VMEM(s, f32) for s in scratch
        ],
        compiler_params=pltpu.CompilerParams(vmem_limit_bytes=limit * 2**20),
    )(*args)


def partner(value, bits):
    return lax.ppermute(value, DOM, [(i, i ^ bits) for i in range(lax.axis_size(DOM))])


def in_group(new):
    p2, p3, p1 = partner(new, 2), partner(new, 3), partner(new, 1)
    return new, p1, p2, p3


def shifts(up, down):
    count = lax.axis_size(DOM)
    forward = [(i, i + 1) for i in range(count - 1)]
    backward = [(i + 1, i) for i in range(count - 1)]
    return lax.ppermute(up, DOM, forward), lax.ppermute(down, DOM, backward)


def cycle(right_side, fine_diagonal, fine_columns, fine_blocks, aggregate_of_node,
         coarse_row_of_aggregate, coarse_diagonal, coarse_columns, coarse_blocks):
    rhs, dia = right_side.T, fine_diagonal.T
    col, blk = fine_columns.T, fine_blocks.transpose(2, 3, 1, 0)
    agg = aggregate_of_node.reshape(8, LANES)
    owner = coarse_row_of_aggregate.reshape(1, 32)
    cdia, cblk = coarse_diagonal.T, coarse_blocks.transpose(2, 3, 0, 1)
    me = lax.axis_index(DOM).astype(i32).reshape(1)
    base = me * ROWS
    wide = WIDE + ROWS + WIDE

    vmem, far = pl.BlockSpec(memory_space=pltpu.VMEM), pl.BlockSpec(memory_space=pltpu.HBM)
    up, down, node_row, dsend = pl.pallas_call(
        pack_kernel,
        name="pack",
        in_specs=[far] * 8,
        out_specs=[vmem] * 4,
        out_shape=[jax.ShapeDtypeStruct(o, f32)
            for o in ((P_ALL, HALO), (P_ALL, HALO), (8, LANES), (NEAR, 80, LANES))],
        scratch_shapes=[
            pltpu.VMEM((3, ROWS), f32), pltpu.VMEM((3, ROWS), f32),
            pltpu.VMEM((2, SLOTS, HALO), i32), pltpu.VMEM((2, 3, 3, SLOTS, HALO), f32),
            pltpu.VMEM((8, LANES), i32), pltpu.VMEM((1, 32), i32),
            pltpu.VMEM((32, SLOTS), i32), pltpu.VMEM((3, 3, 32, SLOTS), f32),
            pltpu.SemaphoreType.DMA((10,)),
        ],
        compiler_params=pltpu.CompilerParams(vmem_limit_bytes=60 * 2**20),
    )(rhs, dia, col, blk, agg, owner, coarse_columns, cblk)
    data = lax.all_to_all(
        dsend, DOM, 0, 0, axis_index_groups=row_groups(), tiled=True
    )
    along_z, along_y = partner(data, 8), partner(data, 32)
    data = (data, along_z, along_y, partner(along_z, 32))
    before, after = shifts(up, down)
    send, first_iter, wrhs, wdia, up2, down2 = call(
        pre_kernel,
        [((LANES, 2, LANES), f32), ((3, wide), f32), ((3, wide), f32), ((3, wide), f32),
         ((3, HALO), f32), ((3, HALO), f32)],
        [base, rhs, dia, col, blk, agg, owner, cdia, before, after],
        scratch=[(3, wide), (3, wide), (8, ROWS)], scalars=1, limit=4,
    )
    before2, after2 = shifts(up2, down2)
    sums = lax.all_to_all(send, DOM, 0, 0, tiled=True)
    peers = ((PEERS, LANES), f32)
    gather = (3, PEERS, LANES)
    square = (LANES, LANES)
    new, crhs, cd, where, passes = call(
        coarse_first_kernel,
        [peers, peers, peers, ((PEERS, 8, LANES), i32), ((8, LANES), i32)],
        [base, sums, *data],
        scratch=[square, gather, ((288, 4096), jnp.bfloat16), ((LANES, 4096), jnp.bfloat16)],
        scalars=1,
    )
    for _ in range(CSWEEPS - 2):
        new, = call(
            coarse_kernel, [peers],
            [base, passes, *in_group(new), crhs, cd, where, *data],
            scratch=[square, square, gather], scalars=1,
        )
    solution, mine = call(
        post_kernel, [((3, ROWS), f32), ((3, 32), f32)],
        [base, *in_group(new), first_iter, wrhs, wdia, col, blk, node_row,
         before, after, before2, after2],
        scratch=[square, square, (3, wide), (3, wide)], scalars=1,
    )
    return solution.T, mine.T


def solution(mesh):
    return jax.shard_map(
        cycle,
        mesh=mesh,
        in_specs=(
            P(DOM, None),
            P(DOM, None),
            P(DOM, None),
            P(DOM, None, None, None),
            P(DOM),
            P(DOM),
            P(DOM, None),
            P(DOM, None),
            P(DOM, None, None, None),
        ),
        out_specs=(P(DOM, None), P(DOM, None)),
        check_vma=False,
    )
```

profile of v0, /device:TPU:103, one launch (start us, length us, event | category | flops | bytes accessed | tf_op | source)
XLA Modules:
  0.0 105.1 jit_solution(12434451521522358879)
XLA Ops:
  0.7 2.5 %pack.1 = (f32[288,256]{1,0:T(8,128)}, f32[288,256]{1,0:T(8,128)}, f32[8,128]{1,0:T(8,128)}, f32[8,80,128]{2,1,0:T(8,128)}) custom-call(f32[3,1024]{1,0:T(4,128)} %bitcast.17, f32[3,1024]{1,0:T(4,128)} %bitcast.19, s32[27,1024]{1,0:T(8,128)} %bitcast.14, f32[3,3,27,1024]{3,2,1,0:T(8,128)} %bitcast.11, s32[8,128]{1,0:T(8,128)} %bitcast.21, s32[1,32]{1,0:T(1,128)} %bitcast.24, ...), custom_call_target="tpu_custom_call" | custom-call | tf_op jit(solution)/shard_map/pack/pallas_call | solution.py:528
  3.2 14.5 %all_to_all.10.rest_0_.rest_7_ = f32[8,80,128]{2,1,0:T(8,128)S(1)} all-to-all(f32[8,80,128]{2,1,0:T(8,128)} %get-tuple-element.22), channel_id=1, replica_groups={{0,6,24,30,96,102,120,126},{1,7,25,31,97,103,121,127},{2,4,26,28,98,100..., dimensions={0} | all-to-all | bytes 655360 | tf_op jit(solution)/shard_map/all_to_all | solution.py:544
  17.6 0.0 collective-permute-start.2
  17.6 6.5 %collective-permute-start = (f32[288,256]{1,0:T(8,128)}, f32[288,256]{1,0:T(8,128)S(1)}, u32[]{:S(2)}, u32[]{:S(2)}) collective-permute-start(f32[288,256]{1,0:T(8,128)} %get-tuple-element.19), channel_id=1, source_target_pairs={{0,1},{1,2},{2,3},{3,4},{4,5},{5,6},{6,7},{7,8},{8,9},{9,10},{10,1... | collective-permute-start | bytes 884744 | tf_op jit(solution)/shard_map/ppermute | solution.py:513
  24.1 1.9 %collective-permute-start.1 = (f32[288,256]{1,0:T(8,128)}, f32[288,256]{1,0:T(8,128)S(1)}, u32[]{:S(2)}, u32[]{:S(2)}) collective-permute-start(f32[288,256]{1,0:T(8,128)} %get-tuple-element.20), channel_id=1, source_target_pairs={{1,0},{2,1},{3,2},{4,3},{5,4},{6,5},{7,6},{8,7},{9,8},{10,9},{11,1... | collective-permute-start | bytes 884744 | tf_op jit(solution)/shard_map/ppermute | solution.py:513
  26.0 0.4 collective-permute-start.3
  26.4 0.0 collective-permute-done.2.rest_1_.rest_8_
  26.4 1.2 %collective-permute-start.4 = (f32[8,80,128]{2,1,0:T(8,128)S(1)}, f32[8,80,128]{2,1,0:T(8,128)S(1)}, u32[]{:S(2)}, u32[]{:S(2)}) collective-permute-start(f32[8,80,128]{2,1,0:T(8,128)S(1)} %collective-permute-done.2.rest_1_.rest_8_), channel_id=1, source_target_pairs={{0,32},{1,33},{2,34},{3,35},{4,36},{5,37},{6,38},{7,39},{8,40},{9,... | collective-permute-start | bytes 983048 | tf_op jit(solution)/shard_map/ppermute | solution.py:501
  27.6 0.5 collective-permute-done.before.rest_10_
  28.1 8.6 %collective-permute-done.1.after.rest_11_ = f32[288,256]{1,0:T(8,128)S(1)} collective-permute-done((f32[288,256]{1,0:T(8,128)}, f32[288,256]{1,0:T(8,128)S(1)}, u32[]{:S(2)}, u32[]{:S(2)}) %collective-permute-start.1) | collective-permute-done | bytes 294944 | tf_op jit(solution)/shard_map/ppermute | solution.py:513
  36.7 2.1 %shard_map.104 = (f32[128,2,128]{2,1,0:T(2,128)S(1)}, f32[3,2048]{1,0:T(4,128)S(1)}, f32[3,2048]{1,0:T(4,128)S(1)}, f32[3,2048]{1,0:T(4,128)S(1)}, f32[3,256]{1,0:T(4,128)S(1)}, /*index=5*/f32[3,256]{1,0:T(4,128)S(1)}) custom-call(s32[1]{0:T(128)} %bitcast.base_ref, f32[3,1024]{1,0:T(4,128)S(1)} %bitcast.18, f32[3,1024]{1,0:T(4,128)S(1)} %bitcast.20, ...), custom_call_target="tpu_custom_call" | custom-call | tf_op jit(solution)/shard_map/pallas_call | solution.py:488
  38.9 14.9 %all_to_all.11.sums = f32[128,2,128]{2,1,0:T(2,128)S(1)} all-to-all(f32[128,2,128]{2,1,0:T(2,128)S(1)} %get-tuple-element.21), channel_id=1, replica_groups=mesh['dom'=128] {'dom'}, dimensions={0} | all-to-all | bytes 262144 | tf_op jit(solution)/shard_map/all_to_all | solution.py:558
  53.7 0.0 collective-permute-done.3.rest_2_.rest_9_
  53.7 0.0 collective-permute-done.4.rest_3_.rest_10_
  53.7 3.7 %shard_map.105 = (f32[32,128]{1,0:T(8,128)S(1)}, f32[32,128]{1,0:T(8,128)S(1)}, f32[32,128]{1,0:T(8,128)S(1)}, s32[32,8,128]{2,1,0:T(8,128)S(1)}, s32[8,128]{1,0:T(8,128)S(1)}) custom-call(s32[1]{0:T(128)} %bitcast.base_ref, f32[128,2,128]{2,1,0:T(2,128)S(1)} %all_to_all.11.sums, f32[8,80,128]{2,1,0:T(8,128)S(1)} %all_to_all.10.rest_0_.rest_7_, ...), custom_call_target="tpu_custom_call" | custom-call | tf_op jit(solution)/shard_map/pallas_call | solution.py:488
  57.4 1.0 collective-permute-start.7
  58.4 1.5 %collective-permute-start.6 = (f32[32,128]{1,0:T(8,128)S(1)}, f32[32,128]{1,0:T(8,128)S(1)}, u32[]{:S(2)}, u32[]{:S(2)}) collective-permute-start(f32[32,128]{1,0:T(8,128)S(1)} %get-tuple-element.24.rest_0_), channel_id=1, source_target_pairs={{0,2},{1,3},{2,0},{3,1},{4,6},{5,7},{6,4},{7,5},{8,10},{9,11},{10,... | collective-permute-start | bytes 49160 | tf_op jit(solution)/shard_map/ppermute | solution.py:501
  59.8 0.0 collective-permute-start.5
  59.8 0.8 collective-permute-done.7.rest_3_
  60.6 0.6 collective-permute-done.6.rest_2_
  61.3 2.1 %shard_map.106.rest_0_ = f32[32,128]{1,0:T(8,128)S(1)} custom-call(s32[1]{0:T(128)} %bitcast.base_ref, s32[8,128]{1,0:T(8,128)S(1)} %get-tuple-element.23.passes, f32[32,128]{1,0:T(8,128)S(1)} %get-tuple-element.24.rest_0_, f32[32,128]{1,0:T(8,128)S(1)} %collective-permute-done.5.rest_1_, f32[32,128]{1,0:T(8,128)S(1)} %collective-permute-done.6.rest_2_, ...), custom_call_target="tpu_custom_call" | custom-call | tf_op jit(solution)/shard_map/pallas_call | solution.py:488
  63.3 1.9 %collective-permute-start.10 = (f32[32,128]{1,0:T(8,128)S(1)}, f32[32,128]{1,0:T(8,128)S(1)}, u32[]{:S(2)}, u32[]{:S(2)}) collective-permute-start(f32[32,128]{1,0:T(8,128)S(1)} %shard_map.106.rest_0_), channel_id=1, source_target_pairs={{0,3},{1,2},{2,1},{3,0},{4,7},{5,6},{6,5},{7,4},{8,11},{9,10},{10,... | collective-permute-start | bytes 49160 | tf_op jit(solution)/shard_map/ppermute | solution.py:501
  65.3 1.7 %collective-permute-start.9 = (f32[32,128]{1,0:T(8,128)S(1)}, f32[32,128]{1,0:T(8,128)S(1)}, u32[]{:S(2)}, u32[]{:S(2)}) collective-permute-start(f32[32,128]{1,0:T(8,128)S(1)} %shard_map.106.rest_0_), channel_id=1, source_target_pairs={{0,2},{1,3},{2,0},{3,1},{4,6},{5,7},{6,4},{7,5},{8,10},{9,11},{10,... | collective-permute-start | bytes 49160 | tf_op jit(solution)/shard_map/ppermute | solution.py:501
  67.0 1.4 %collective-permute-done.9.rest_2_ = f32[32,128]{1,0:T(8,128)S(1)} collective-permute-done((f32[32,128]{1,0:T(8,128)S(1)}, f32[32,128]{1,0:T(8,128)S(1)}, u32[]{:S(2)}, u32[]{:S(2)}) %collective-permute-start.9) | collective-permute-done | bytes 16416 | tf_op jit(solution)/shard_map/ppermute | solution.py:501
  68.4 0.0 collective-permute-done.8.rest_1_
  68.4 2.1 %shard_map.107.rest_0_ = f32[32,128]{1,0:T(8,128)S(1)} custom-call(s32[1]{0:T(128)} %bitcast.base_ref, s32[8,128]{1,0:T(8,128)S(1)} %get-tuple-element.23.passes, f32[32,128]{1,0:T(8,128)S(1)} %shard_map.106.rest_0_, f32[32,128]{1,0:T(8,128)S(1)} %collective-permute-done.8.rest_1_, f32[32,128]{1,0:T(8,128)S(1)} %collective-permute-done.9.rest_2_, ...), custom_call_target="tpu_custom_call" | custom-call | tf_op jit(solution)/shard_map/pallas_call | solution.py:488
  70.5 0.0 copy-start.5
  70.5 1.2 %collective-permute-start.13 = (f32[32,128]{1,0:T(8,128)S(1)}, f32[32,128]{1,0:T(8,128)S(1)}, u32[]{:S(2)}, u32[]{:S(2)}) collective-permute-start(f32[32,128]{1,0:T(8,128)S(1)} %shard_map.107.rest_0_), channel_id=1, source_target_pairs={{0,3},{1,2},{2,1},{3,0},{4,7},{5,6},{6,5},{7,4},{8,11},{9,10},{10,... | collective-permute-start | bytes 49160 | tf_op jit(solution)/shard_map/ppermute | solution.py:501
  71.7 2.2 %collective-permute-start.12 = (f32[32,128]{1,0:T(8,128)S(1)}, f32[32,128]{1,0:T(8,128)S(1)}, u32[]{:S(2)}, u32[]{:S(2)}) collective-permute-start(f32[32,128]{1,0:T(8,128)S(1)} %shard_map.107.rest_0_), channel_id=1, source_target_pairs={{0,2},{1,3},{2,0},{3,1},{4,6},{5,7},{6,4},{7,5},{8,10},{9,11},{10,... | collective-permute-start | bytes 49160 | tf_op jit(solution)/shard_map/ppermute | solution.py:501
  73.9 1.4 %collective-permute-done.12.rest_2_ = f32[32,128]{1,0:T(8,128)S(1)} collective-permute-done((f32[32,128]{1,0:T(8,128)S(1)}, f32[32,128]{1,0:T(8,128)S(1)}, u32[]{:S(2)}, u32[]{:S(2)}) %collective-permute-start.12) | collective-permute-done | bytes 16416 | tf_op jit(solution)/shard_map/ppermute | solution.py:501
  75.3 0.0 collective-permute-done.11.rest_1_
  75.3 2.1 %shard_map.108.rest_0_ = f32[32,128]{1,0:T(8,128)S(1)} custom-call(s32[1]{0:T(128)} %bitcast.base_ref, s32[8,128]{1,0:T(8,128)S(1)} %get-tuple-element.23.passes, f32[32,128]{1,0:T(8,128)S(1)} %shard_map.107.rest_0_, f32[32,128]{1,0:T(8,128)S(1)} %collective-permute-done.11.rest_1_, f32[32,128]{1,0:T(8,128)S(1)} %collective-permute-done.12.rest_2_, ...), custom_call_target="tpu_custom_call" | custom-call | tf_op jit(solution)/shard_map/pallas_call | solution.py:488
  77.4 1.0 collective-permute-start.16
  78.4 2.2 %collective-permute-start.15 = (f32[32,128]{1,0:T(8,128)S(1)}, f32[32,128]{1,0:T(8,128)S(1)}, u32[]{:S(2)}, u32[]{:S(2)}) collective-permute-start(f32[32,128]{1,0:T(8,128)S(1)} %shard_map.108.rest_0_), channel_id=1, source_target_pairs={{0,2},{1,3},{2,0},{3,1},{4,6},{5,7},{6,4},{7,5},{8,10},{9,11},{10,... | collective-permute-start | bytes 49160 | tf_op jit(solution)/shard_map/ppermute | solution.py:501
  80.6 0.0 collective-permute-start.14
  80.6 0.0 collective-permute-done.16.rest_3_
  80.6 1.4 %collective-permute-done.15.rest_2_ = f32[32,128]{1,0:T(8,128)S(1)} collective-permute-done((f32[32,128]{1,0:T(8,128)S(1)}, f32[32,128]{1,0:T(8,128)S(1)}, u32[]{:S(2)}, u32[]{:S(2)}) %collective-permute-start.15) | collective-permute-done | bytes 16416 | tf_op jit(solution)/shard_map/ppermute | solution.py:501
  82.0 0.0 collective-permute-done.14.rest_1_
  82.0 2.1 %shard_map.109.rest_0_ = f32[32,128]{1,0:T(8,128)S(1)} custom-call(s32[1]{0:T(128)} %bitcast.base_ref, s32[8,128]{1,0:T(8,128)S(1)} %get-tuple-element.23.passes, f32[32,128]{1,0:T(8,128)S(1)} %shard_map.108.rest_0_, f32[32,128]{1,0:T(8,128)S(1)} %collective-permute-done.14.rest_1_, f32[32,128]{1,0:T(8,128)S(1)} %collective-permute-done.15.rest_2_, ...), custom_call_target="tpu_custom_call" | custom-call | tf_op jit(solution)/shard_map/pallas_call | solution.py:488
  84.1 1.2 %collective-permute-start.19 = (f32[32,128]{1,0:T(8,128)S(1)}, f32[32,128]{1,0:T(8,128)S(1)}, u32[]{:S(2)}, u32[]{:S(2)}) collective-permute-start(f32[32,128]{1,0:T(8,128)S(1)} %shard_map.109.rest_0_), channel_id=1, source_target_pairs={{0,3},{1,2},{2,1},{3,0},{4,7},{5,6},{6,5},{7,4},{8,11},{9,10},{10,... | collective-permute-start | bytes 49160 | tf_op jit(solution)/shard_map/ppermute | solution.py:501
  85.3 2.2 %collective-permute-start.18 = (f32[32,128]{1,0:T(8,128)S(1)}, f32[32,128]{1,0:T(8,128)S(1)}, u32[]{:S(2)}, u32[]{:S(2)}) collective-permute-start(f32[32,128]{1,0:T(8,128)S(1)} %shard_map.109.rest_0_), channel_id=1, source_target_pairs={{0,2},{1,3},{2,0},{3,1},{4,6},{5,7},{6,4},{7,5},{8,10},{9,11},{10,... | collective-permute-start | bytes 49160 | tf_op jit(solution)/shard_map/ppermute | solution.py:501
  87.5 0.0 collective-permute-start.17
  87.5 5.8 %collective-permute-start.20 = (f32[3,256]{1,0:T(4,128)S(1)}, f32[3,256]{1,0:T(4,128)S(1)}, u32[]{:S(2)}, u32[]{:S(2)}) collective-permute-start(f32[3,256]{1,0:T(4,128)S(1)} %get-tuple-element.32), channel_id=1, source_target_pairs={{0,1},{1,2},{2,3},{3,4},{4,5},{5,6},{6,7},{7,8},{8,9},{9,10},{10,1... | collective-permute-start | bytes 9224 | tf_op jit(solution)/shard_map/ppermute | solution.py:513
  93.3 1.9 %collective-permute-start.21 = (f32[3,256]{1,0:T(4,128)S(1)}, f32[3,256]{1,0:T(4,128)S(1)}, u32[]{:S(2)}, u32[]{:S(2)}) collective-permute-start(f32[3,256]{1,0:T(4,128)S(1)} %get-tuple-element.33), channel_id=1, source_target_pairs={{1,0},{2,1},{3,2},{4,3},{5,4},{6,5},{7,6},{8,7},{9,8},{10,9},{11,1... | collective-permute-start | bytes 9224 | tf_op jit(solution)/shard_map/ppermute | solution.py:513
  95.2 7.2 %collective-permute-done.21.rest_13_ = f32[3,256]{1,0:T(4,128)S(1)} collective-permute-done((f32[3,256]{1,0:T(4,128)S(1)}, f32[3,256]{1,0:T(4,128)S(1)}, u32[]{:S(2)}, u32[]{:S(2)}) %collective-permute-start.21) | collective-permute-done | bytes 3104 | tf_op jit(solution)/shard_map/ppermute | solution.py:513
  102.4 0.0 collective-permute-done.19.rest_3_
  102.4 0.0 collective-permute-done.18.rest_2_
  102.5 2.7 %shard_map.110 = (f32[3,1024]{1,0:T(4,128)}, f32[3,32]{1,0:T(4,128)}) custom-call(s32[1]{0:T(128)} %bitcast.base_ref, f32[32,128]{1,0:T(8,128)S(1)} %shard_map.109.rest_0_, f32[32,128]{1,0:T(8,128)S(1)} %collective-permute-done.17.rest_1_, f32[32,128]{1,0:T(8,128)S(1)} %collective-permute-done.18.rest_2_, f32[32,128]{1,0:T(8,128)S(1)} %collective-permute-done.19.rest_3_, ...), custom_call_target="tpu_custom_call" | custom-call | tf_op jit(solution)/shard_map/pallas_call | solution.py:488
  (22 shorter events, 0.1 us)
Async XLA Ops:
  0.6 36.1 %copy-start.7 = (s32[32]{0:T(128)S(1)}, s32[32]{0:T(128)}, u32[]{:S(2)}) copy-start(s32[32]{0:T(128)} %param.14) | copy-start | bytes 388
  0.6 36.0 %copy-start.4 = (s32[1024]{0:T(1024)S(1)}, s32[1024]{0:T(1024)}, u32[]{:S(2)}) copy-start(s32[1024]{0:T(1024)} %param.13) | copy-start | bytes 12292
  0.7 36.0 %copy-start = (f32[1024,27,3,3]{0,1,3,2:T(8,128)S(1)}, f32[1024,27,3,3]{0,1,3,2:T(8,128)}, u32[]{:S(2)}) copy-start(f32[1024,27,3,3]{0,1,3,2:T(8,128)} %param.12) | copy-start | bytes 2985988
  0.7 36.0 %copy-start.1 = (s32[1024,27]{0,1:T(8,128)S(1)}, s32[1024,27]{0,1:T(8,128)}, u32[]{:S(2)}) copy-start(s32[1024,27]{0,1:T(8,128)} %param.11) | copy-start | bytes 331780
  0.7 36.0 %copy-start.3 = (f32[1024,3]{0,1:T(4,128)S(1)}, f32[1024,3]{0,1:T(4,128)}, u32[]{:S(2)}) copy-start(f32[1024,3]{0,1:T(4,128)} %param.10) | copy-start | bytes 36868
  0.7 36.0 %copy-start.2 = (f32[1024,3]{0,1:T(4,128)S(1)}, f32[1024,3]{0,1:T(4,128)}, u32[]{:S(2)}) copy-start(f32[1024,3]{0,1:T(4,128)} %param.9) | copy-start | bytes 36868
  0.7 36.0 %copy-start.6 = (f32[32,3]{0,1:T(4,128)S(1)}, f32[32,3]{0,1:T(4,128)}, u32[]{:S(2)}) copy-start(f32[32,3]{0,1:T(4,128)} %param.15) | copy-start | bytes 1156
  17.6 8.8 %collective-permute-start.2 = (f32[8,80,128]{2,1,0:T(8,128)S(1)}, f32[8,80,128]{2,1,0:T(8,128)S(1)}, u32[]{:S(2)}, u32[]{:S(2)}) collective-permute-start(f32[8,80,128]{2,1,0:T(8,128)S(1)} %all_to_all.10.rest_0_.rest_7_), channel_id=1, source_target_pairs={{0,8},{1,9},{2,10},{3,11},{4,12},{5,13},{6,14},{7,15},{8,0},{9,1},... | collective-permute-start | bytes 983048 | tf_op jit(solution)/shard_map/ppermute | solution.py:501
  17.6 10.5 %collective-permute-start = (f32[288,256]{1,0:T(8,128)}, f32[288,256]{1,0:T(8,128)S(1)}, u32[]{:S(2)}, u32[]{:S(2)}) collective-permute-start(f32[288,256]{1,0:T(8,128)} %get-tuple-element.19), channel_id=1, source_target_pairs={{0,1},{1,2},{2,3},{3,4},{4,5},{5,6},{6,7},{7,8},{8,9},{9,10},{10,1... | collective-permute-start | bytes 884744 | tf_op jit(solution)/shard_map/ppermute | solution.py:513
  24.1 12.6 %collective-permute-start.1 = (f32[288,256]{1,0:T(8,128)}, f32[288,256]{1,0:T(8,128)S(1)}, u32[]{:S(2)}, u32[]{:S(2)}) collective-permute-start(f32[288,256]{1,0:T(8,128)} %get-tuple-element.20), channel_id=1, source_target_pairs={{1,0},{2,1},{3,2},{4,3},{5,4},{6,5},{7,6},{8,7},{9,8},{10,9},{11,1... | collective-permute-start | bytes 884744 | tf_op jit(solution)/shard_map/ppermute | solution.py:513
  26.0 27.7 %collective-permute-start.3 = (f32[8,80,128]{2,1,0:T(8,128)S(1)}, f32[8,80,128]{2,1,0:T(8,128)S(1)}, u32[]{:S(2)}, u32[]{:S(2)}) collective-permute-start(f32[8,80,128]{2,1,0:T(8,128)S(1)} %all_to_all.10.rest_0_.rest_7_), channel_id=1, source_target_pairs={{0,32},{1,33},{2,34},{3,35},{4,36},{5,37},{6,38},{7,39},{8,40},{9,... | collective-permute-start | bytes 983048 | tf_op jit(solution)/shard_map/ppermute | solution.py:501
  26.4 27.3 %collective-permute-start.4 = (f32[8,80,128]{2,1,0:T(8,128)S(1)}, f32[8,80,128]{2,1,0:T(8,128)S(1)}, u32[]{:S(2)}, u32[]{:S(2)}) collective-permute-start(f32[8,80,128]{2,1,0:T(8,128)S(1)} %collective-permute-done.2.rest_1_.rest_8_), channel_id=1, source_target_pairs={{0,32},{1,33},{2,34},{3,35},{4,36},{5,37},{6,38},{7,39},{8,40},{9,... | collective-permute-start | bytes 983048 | tf_op jit(solution)/shard_map/ppermute | solution.py:501
  57.4 3.2 %collective-permute-start.7 = (f32[32,128]{1,0:T(8,128)S(1)}, f32[32,128]{1,0:T(8,128)S(1)}, u32[]{:S(2)}, u32[]{:S(2)}) collective-permute-start(f32[32,128]{1,0:T(8,128)S(1)} %get-tuple-element.24.rest_0_), channel_id=1, source_target_pairs={{0,3},{1,2},{2,1},{3,0},{4,7},{5,6},{6,5},{7,4},{8,11},{9,10},{10,... | collective-permute-start | bytes 49160 | tf_op jit(solution)/shard_map/ppermute | solution.py:501
  58.4 2.9 %collective-permute-start.6 = (f32[32,128]{1,0:T(8,128)S(1)}, f32[32,128]{1,0:T(8,128)S(1)}, u32[]{:S(2)}, u32[]{:S(2)}) collective-permute-start(f32[32,128]{1,0:T(8,128)S(1)} %get-tuple-element.24.rest_0_), channel_id=1, source_target_pairs={{0,2},{1,3},{2,0},{3,1},{4,6},{5,7},{6,4},{7,5},{8,10},{9,11},{10,... | collective-permute-start | bytes 49160 | tf_op jit(solution)/shard_map/ppermute | solution.py:501
  59.8 1.4 %collective-permute-start.5 = (f32[32,128]{1,0:T(8,128)S(1)}, f32[32,128]{1,0:T(8,128)S(1)}, u32[]{:S(2)}, u32[]{:S(2)}) collective-permute-start(f32[32,128]{1,0:T(8,128)S(1)} %get-tuple-element.24.rest_0_), channel_id=1, source_target_pairs={{0,1},{1,0},{2,3},{3,2},{4,5},{5,4},{6,7},{7,6},{8,9},{9,8},{10,11... | collective-permute-start | bytes 49160 | tf_op jit(solution)/shard_map/ppermute | solution.py:501
  63.3 3.6 %collective-permute-start.10 = (f32[32,128]{1,0:T(8,128)S(1)}, f32[32,128]{1,0:T(8,128)S(1)}, u32[]{:S(2)}, u32[]{:S(2)}) collective-permute-start(f32[32,128]{1,0:T(8,128)S(1)} %shard_map.106.rest_0_), channel_id=1, source_target_pairs={{0,3},{1,2},{2,1},{3,0},{4,7},{5,6},{6,5},{7,4},{8,11},{9,10},{10,... | collective-permute-start | bytes 49160 | tf_op jit(solution)/shard_map/ppermute | solution.py:501
  65.3 3.1 %collective-permute-start.9 = (f32[32,128]{1,0:T(8,128)S(1)}, f32[32,128]{1,0:T(8,128)S(1)}, u32[]{:S(2)}, u32[]{:S(2)}) collective-permute-start(f32[32,128]{1,0:T(8,128)S(1)} %shard_map.106.rest_0_), channel_id=1, source_target_pairs={{0,2},{1,3},{2,0},{3,1},{4,6},{5,7},{6,4},{7,5},{8,10},{9,11},{10,... | collective-permute-start | bytes 49160 | tf_op jit(solution)/shard_map/ppermute | solution.py:501
  67.0 1.4 %collective-permute-start.8 = (f32[32,128]{1,0:T(8,128)S(1)}, f32[32,128]{1,0:T(8,128)S(1)}, u32[]{:S(2)}, u32[]{:S(2)}) collective-permute-start(f32[32,128]{1,0:T(8,128)S(1)} %shard_map.106.rest_0_), channel_id=1, source_target_pairs={{0,1},{1,0},{2,3},{3,2},{4,5},{5,4},{6,7},{7,6},{8,9},{9,8},{10,11... | collective-permute-start | bytes 49160 | tf_op jit(solution)/shard_map/ppermute | solution.py:501
  70.5 32.0 %copy-start.5 = (f32[8,128]{1,0:T(8,128)S(1)}, f32[8,128]{1,0:T(8,128)}, u32[]{:S(2)}) copy-start(f32[8,128]{1,0:T(8,128)} %get-tuple-element.31.rest_9_) | copy-start | bytes 12292
  70.5 3.4 %collective-permute-start.13 = (f32[32,128]{1,0:T(8,128)S(1)}, f32[32,128]{1,0:T(8,128)S(1)}, u32[]{:S(2)}, u32[]{:S(2)}) collective-permute-start(f32[32,128]{1,0:T(8,128)S(1)} %shard_map.107.rest_0_), channel_id=1, source_target_pairs={{0,3},{1,2},{2,1},{3,0},{4,7},{5,6},{6,5},{7,4},{8,11},{9,10},{10,... | collective-permute-start | bytes 49160 | tf_op jit(solution)/shard_map/ppermute | solution.py:501
  71.7 3.6 %collective-permute-start.12 = (f32[32,128]{1,0:T(8,128)S(1)}, f32[32,128]{1,0:T(8,128)S(1)}, u32[]{:S(2)}, u32[]{:S(2)}) collective-permute-start(f32[32,128]{1,0:T(8,128)S(1)} %shard_map.107.rest_0_), channel_id=1, source_target_pairs={{0,2},{1,3},{2,0},{3,1},{4,6},{5,7},{6,4},{7,5},{8,10},{9,11},{10,... | collective-permute-start | bytes 49160 | tf_op jit(solution)/shard_map/ppermute | solution.py:501
  73.9 1.4 %collective-permute-start.11 = (f32[32,128]{1,0:T(8,128)S(1)}, f32[32,128]{1,0:T(8,128)S(1)}, u32[]{:S(2)}, u32[]{:S(2)}) collective-permute-start(f32[32,128]{1,0:T(8,128)S(1)} %shard_map.107.rest_0_), channel_id=1, source_target_pairs={{0,1},{1,0},{2,3},{3,2},{4,5},{5,4},{6,7},{7,6},{8,9},{9,8},{10,11... | collective-permute-start | bytes 49160 | tf_op jit(solution)/shard_map/ppermute | solution.py:501
  77.4 3.2 %collective-permute-start.16 = (f32[32,128]{1,0:T(8,128)S(1)}, f32[32,128]{1,0:T(8,128)S(1)}, u32[]{:S(2)}, u32[]{:S(2)}) collective-permute-start(f32[32,128]{1,0:T(8,128)S(1)} %shard_map.108.rest_0_), channel_id=1, source_target_pairs={{0,3},{1,2},{2,1},{3,0},{4,7},{5,6},{6,5},{7,4},{8,11},{9,10},{10,... | collective-permute-start | bytes 49160 | tf_op jit(solution)/shard_map/ppermute | solution.py:501
  78.4 3.6 %collective-permute-start.15 = (f32[32,128]{1,0:T(8,128)S(1)}, f32[32,128]{1,0:T(8,128)S(1)}, u32[]{:S(2)}, u32[]{:S(2)}) collective-permute-start(f32[32,128]{1,0:T(8,128)S(1)} %shard_map.108.rest_0_), channel_id=1, source_target_pairs={{0,2},{1,3},{2,0},{3,1},{4,6},{5,7},{6,4},{7,5},{8,10},{9,11},{10,... | collective-permute-start | bytes 49160 | tf_op jit(solution)/shard_map/ppermute | solution.py:501
  80.6 1.4 %collective-permute-start.14 = (f32[32,128]{1,0:T(8,128)S(1)}, f32[32,128]{1,0:T(8,128)S(1)}, u32[]{:S(2)}, u32[]{:S(2)}) collective-permute-start(f32[32,128]{1,0:T(8,128)S(1)} %shard_map.108.rest_0_), channel_id=1, source_target_pairs={{0,1},{1,0},{2,3},{3,2},{4,5},{5,4},{6,7},{7,6},{8,9},{9,8},{10,11... | collective-permute-start | bytes 49160 | tf_op jit(solution)/shard_map/ppermute | solution.py:501
  84.1 18.3 %collective-permute-start.19 = (f32[32,128]{1,0:T(8,128)S(1)}, f32[32,128]{1,0:T(8,128)S(1)}, u32[]{:S(2)}, u32[]{:S(2)}) collective-permute-start(f32[32,128]{1,0:T(8,128)S(1)} %shard_map.109.rest_0_), channel_id=1, source_target_pairs={{0,3},{1,2},{2,1},{3,0},{4,7},{5,6},{6,5},{7,4},{8,11},{9,10},{10,... | collective-permute-start | bytes 49160 | tf_op jit(solution)/shard_map/ppermute | solution.py:501
  85.3 17.1 %collective-permute-start.18 = (f32[32,128]{1,0:T(8,128)S(1)}, f32[32,128]{1,0:T(8,128)S(1)}, u32[]{:S(2)}, u32[]{:S(2)}) collective-permute-start(f32[32,128]{1,0:T(8,128)S(1)} %shard_map.109.rest_0_), channel_id=1, source_target_pairs={{0,2},{1,3},{2,0},{3,1},{4,6},{5,7},{6,4},{7,5},{8,10},{9,11},{10,... | collective-permute-start | bytes 49160 | tf_op jit(solution)/shard_map/ppermute | solution.py:501
  87.5 15.0 %collective-permute-start.17 = (f32[32,128]{1,0:T(8,128)S(1)}, f32[32,128]{1,0:T(8,128)S(1)}, u32[]{:S(2)}, u32[]{:S(2)}) collective-permute-start(f32[32,128]{1,0:T(8,128)S(1)} %shard_map.109.rest_0_), channel_id=1, source_target_pairs={{0,1},{1,0},{2,3},{3,2},{4,5},{5,4},{6,7},{7,6},{8,9},{9,8},{10,11... | collective-permute-start | bytes 49160 | tf_op jit(solution)/shard_map/ppermute | solution.py:501
  87.5 7.7 %collective-permute-start.20 = (f32[3,256]{1,0:T(4,128)S(1)}, f32[3,256]{1,0:T(4,128)S(1)}, u32[]{:S(2)}, u32[]{:S(2)}) collective-permute-start(f32[3,256]{1,0:T(4,128)S(1)} %get-tuple-element.32), channel_id=1, source_target_pairs={{0,1},{1,2},{2,3},{3,4},{4,5},{5,6},{6,7},{7,8},{8,9},{9,10},{10,1... | collective-permute-start | bytes 9224 | tf_op jit(solution)/shard_map/ppermute | solution.py:513
  93.3 9.1 %collective-permute-start.21 = (f32[3,256]{1,0:T(4,128)S(1)}, f32[3,256]{1,0:T(4,128)S(1)}, u32[]{:S(2)}, u32[]{:S(2)}) collective-permute-start(f32[3,256]{1,0:T(4,128)S(1)} %get-tuple-element.33), channel_id=1, source_target_pairs={{1,0},{2,1},{3,2},{4,3},{5,4},{6,5},{7,6},{8,7},{9,8},{10,9},{11,1... | collective-permute-start | bytes 9224 | tf_op jit(solution)/shard_map/ppermute | solution.py:513
where the time goes:
time: 105 us
  starting transfers between devices  33.7 us (32%)
  blocking collectives  29.3 us (28%)
  waiting for transfers between devices  22 us (21%)
  Pallas kernels  19.2 us (18%)
    ppermute x18, starting transfers between devices, partner(): lax.ppermute(value, DOM, [(i, i ^ bits) for i in range(lax.axis_size(DOM))])  17.6 us
    pallas_call x7, Pallas kernels, call(): pl.pallas_call(kernel, in_specs=[smem] * scalars + [vmem] * (len(args) -...  16.8 us
    ppermute x4, waiting for transfers between devices, shifts(): return (lax.ppermute(up, DOM, forward), lax.ppermute(down, DOM, backward))  16.3 us
    ppermute x4, starting transfers between devices, shifts(): return (lax.ppermute(up, DOM, forward), lax.ppermute(down, DOM, backward))  16.1 us
    all_to_all x1, blocking collectives, cycle(): sums = lax.all_to_all(send, DOM, 0, 0, tiled=True)  14.9 us
    all_to_all x1, blocking collectives, cycle(): lax.all_to_all(dsend, DOM, 0, 0, axis_index_groups=row_groups(), tiled=True)  14.5 us
    ppermute x18, waiting for transfers between devices, partner(): lax.ppermute(value, DOM, [(i, i ^ bits) for i in range(lax.axis_size(DOM))])  5.68 us
    pallas_call x1, Pallas kernels, cycle(): pl.pallas_call(pack_kernel, name='pack', in_specs=[far] * 8, out_specs=[v...  2.47 us
  transfers between devices with their start and end apart: 22, of which 8 were waited for; matrix products, arithmetic and copies ran while one was open for 0% of the time, Pallas kernels for 2%

commit v1 on v0

--- a/solution.py
+++ b/solution.py
@@ -9,7 +9,7 @@
 DOM = "dom"
 PEERS = 32
 NEAR = 8
-PARTS = PEERS // NEAR
+PARTS = 5
 PIECES = 128 // PEERS
 UNROLL = 8
 CSWEEPS = 6
@@ -337,9 +337,9 @@
                 for j in range(3):
                     near[j] = jnp.where(here, picked(rows[j][v], lane), near[j])
             for i in range(3):
-                a = data[d // NEAR][d % NEAR, lanes8(3 * i), :] * near[0]
-                a = a + data[d // NEAR][d % NEAR, lanes8(3 * i + 1), :] * near[1]
-                a = a + data[d // NEAR][d % NEAR, lanes8(3 * i + 2), :] * near[2]
+                a = rows_of(data, d)[lanes8(3 * i), :] * near[0]
+                a = a + rows_of(data, d)[lanes8(3 * i + 1), :] * near[1]
+                a = a + rows_of(data, d)[lanes8(3 * i + 2), :] * near[2]
                 gather[i, d : d + 1, :] += jnp.sum(a, axis=0, keepdims=True)
         return carry
 
@@ -350,6 +350,11 @@
         s = s + pltpu.roll(s, 64, axis=1)
         parts.append(s + pltpu.roll(s, 32, axis=1))
     return own + damping * (rhs - (dia * own - spread(parts))) / dia
+
+
+def rows_of(data, d):
+    part, at = (d // NEAR, d % NEAR) if d < 24 else (3 + (d - 24) // 4, d % 4)
+    return data[part].at[at]
 
 
 def lanes8(m):
@@ -400,7 +405,7 @@
     sub = lax.broadcasted_iota(i32, (8, LANES), 0)
     most = jnp.zeros((8, LANES), i32)
     for d in range(PEERS):
-        c = data[d // NEAR][d % NEAR, 72:80, :].astype(i32)
+        c = rows_of(data, d)[72:80, :].astype(i32)
         off = lax.bitwise_and(sub - c, 7)
         most = jnp.maximum(most, off)
         at = lane_of_device(lax.shift_right_logical(c, 5), me)
@@ -545,7 +550,8 @@
         dsend, DOM, 0, 0, axis_index_groups=row_groups(), tiled=True
     )
     along_z, along_y = partner(data, 8), partner(data, 32)
-    data = (data, along_z, along_y, partner(along_z, 32))
+    far_y, far_z = partner(along_z[:4], 32), partner(along_y[4:], 8)
+    data = (data, along_z, along_y, far_y, far_z)
     before, after = shifts(up, down)
     send, first_iter, wrhs, wdia, up2, down2 = call(
         pre_kernel,

time: 105 us -> 106 us (level)
  blocking collectives: 29.3 us -> 26.8 us
  starting transfers between devices: 33.7 us -> 35.5 us
    ppermute x4, starting transfers between devices: 16.1 us -> 19.2 us  [shifts(): return (lax.ppermute(up, DOM, forward), lax.ppermute(down, DOM, backward))]
    all_to_all x1, blocking collectives: 14.9 us -> 12.3 us  [cycle(): sums = lax.all_to_all(send, DOM, 0, 0, tiled=True)]
    ppermute x18 -> x19, starting transfers between devices: 17.6 us -> 16.3 us  [partner(): lax.ppermute(value, DOM, [(i, i ^ bits) for i in range(lax.axis_size(DOM))])]
    ppermute x18 -> x19, waiting for transfers between devices: 5.68 us -> 5.68 us  [partner(): lax.ppermute(value, DOM, [(i, i ^ bits) for i in range(lax.axis_size(DOM))])]
  transfers between devices with their start and end apart: 22 -> 23, of which waited for: 8 -> 8; matrix products, arithmetic and copies ran while one was open for 0% -> 1% of each run, Pallas kernels for 2% -> 2%
where the time goes in v1:
time: 106 us
  starting transfers between devices  35.5 us (33%)
  blocking collectives  26.8 us (25%)
  waiting for transfers between devices  22.6 us (21%)
  Pallas kernels  19.2 us (18%)
    ppermute x4, starting transfers between devices, shifts(): return (lax.ppermute(up, DOM, forward), lax.ppermute(down, DOM, backward))  19.2 us
    ppermute x4, waiting for transfers between devices, shifts(): return (lax.ppermute(up, DOM, forward), lax.ppermute(down, DOM, backward))  16.9 us
    pallas_call x7, Pallas kernels, call(): pl.pallas_call(kernel, in_specs=[smem] * scalars + [vmem] * (len(args) -...  16.8 us
    ppermute x19, starting transfers between devices, partner(): lax.ppermute(value, DOM, [(i, i ^ bits) for i in range(lax.axis_size(DOM))])  16.3 us
    all_to_all x1, blocking collectives, cycle(): lax.all_to_all(dsend, DOM, 0, 0, axis_index_groups=row_groups(), tiled=True)  14.5 us
    all_to_all x1, blocking collectives, cycle(): sums = lax.all_to_all(send, DOM, 0, 0, tiled=True)  12.3 us
    ppermute x19, waiting for transfers between devices, partner(): lax.ppermute(value, DOM, [(i, i ^ bits) for i in range(lax.axis_size(DOM))])  5.68 us
    pallas_call x1, Pallas kernels, cycle(): pl.pallas_call(pack_kernel, name='pack', in_specs=[far] * 8, out_specs=[v...  2.47 us
  transfers between devices with their start and end apart: 23, of which 8 were waited for; matrix products, arithmetic and copies ran while one was open for 1% of the time, Pallas kernels for 2%

profile of v1, /device:TPU:103, one launch (start us, length us, event | category | flops | bytes accessed | tf_op | source)
XLA Modules:
  0.0 105.8 jit_solution(13308014887191082704)
XLA Ops:
  0.7 2.5 %pack.1 = (f32[288,256]{1,0:T(8,128)}, f32[288,256]{1,0:T(8,128)}, f32[8,128]{1,0:T(8,128)}, f32[8,80,128]{2,1,0:T(8,128)}) custom-call(f32[3,1024]{1,0:T(4,128)} %bitcast.17, f32[3,1024]{1,0:T(4,128)} %bitcast.19, s32[27,1024]{1,0:T(8,128)} %bitcast.14, f32[3,3,27,1024]{3,2,1,0:T(8,128)} %bitcast.11, s32[8,128]{1,0:T(8,128)} %bitcast.21, s32[1,32]{1,0:T(1,128)} %bitcast.24, ...), custom_call_target="tpu_custom_call" | custom-call | tf_op jit(solution)/shard_map/pack/pallas_call | solution.py:533
  3.2 14.5 %all_to_all.10.rest_0_.rest_7_ = f32[8,80,128]{2,1,0:T(8,128)S(1)} all-to-all(f32[8,80,128]{2,1,0:T(8,128)} %get-tuple-element.22), channel_id=1, replica_groups={{0,6,24,30,96,102,120,126},{1,7,25,31,97,103,121,127},{2,4,26,28,98,100..., dimensions={0} | all-to-all | bytes 655360 | tf_op jit(solution)/shard_map/all_to_all | solution.py:549
  17.6 9.6 %collective-permute-start = (f32[288,256]{1,0:T(8,128)}, f32[288,256]{1,0:T(8,128)S(1)}, u32[]{:S(2)}, u32[]{:S(2)}) collective-permute-start(f32[288,256]{1,0:T(8,128)} %get-tuple-element.19), channel_id=1, source_target_pairs={{0,1},{1,2},{2,3},{3,4},{4,5},{5,6},{6,7},{7,8},{8,9},{9,10},{10,1... | collective-permute-start | bytes 884744 | tf_op jit(solution)/shard_map/ppermute | solution.py:518
  27.2 1.9 %collective-permute-start.1 = (f32[288,256]{1,0:T(8,128)}, f32[288,256]{1,0:T(8,128)S(1)}, u32[]{:S(2)}, u32[]{:S(2)}) collective-permute-start(f32[288,256]{1,0:T(8,128)} %get-tuple-element.20), channel_id=1, source_target_pairs={{1,0},{2,1},{3,2},{4,3},{5,4},{6,5},{7,6},{8,7},{9,8},{10,9},{11,1... | collective-permute-start | bytes 884744 | tf_op jit(solution)/shard_map/ppermute | solution.py:518
  29.1 0.0 collective-permute-done.3.rest_2_.rest_9_
  29.2 0.1 collective-permute-start.5
  29.3 0.7 slice.8
  29.9 0.0 collective-permute-start.4
  29.9 1.2 %collective-permute-done.before.rest_10_ = f32[288,256]{1,0:T(8,128)S(1)} collective-permute-done((f32[288,256]{1,0:T(8,128)}, f32[288,256]{1,0:T(8,128)S(1)}, u32[]{:S(2)}, u32[]{:S(2)}) %collective-permute-start) | collective-permute-done | bytes 294944 | tf_op jit(solution)/shard_map/ppermute | solution.py:518
  31.2 8.5 %collective-permute-done.1.after.rest_11_ = f32[288,256]{1,0:T(8,128)S(1)} collective-permute-done((f32[288,256]{1,0:T(8,128)}, f32[288,256]{1,0:T(8,128)S(1)}, u32[]{:S(2)}, u32[]{:S(2)}) %collective-permute-start.1) | collective-permute-done | bytes 294944 | tf_op jit(solution)/shard_map/ppermute | solution.py:518
  39.7 2.1 %shard_map.104 = (f32[128,2,128]{2,1,0:T(2,128)S(1)}, f32[3,2048]{1,0:T(4,128)S(1)}, f32[3,2048]{1,0:T(4,128)S(1)}, f32[3,2048]{1,0:T(4,128)S(1)}, f32[3,256]{1,0:T(4,128)S(1)}, /*index=5*/f32[3,256]{1,0:T(4,128)S(1)}) custom-call(s32[1]{0:T(128)} %bitcast.base_ref, f32[3,1024]{1,0:T(4,128)S(1)} %bitcast.18, f32[3,1024]{1,0:T(4,128)S(1)} %bitcast.20, ...), custom_call_target="tpu_custom_call" | custom-call | tf_op jit(solution)/shard_map/pallas_call | solution.py:493
  41.9 12.3 %all_to_all.11.sums = f32[128,2,128]{2,1,0:T(2,128)S(1)} all-to-all(f32[128,2,128]{2,1,0:T(2,128)S(1)} %get-tuple-element.21), channel_id=1, replica_groups=mesh['dom'=128] {'dom'}, dimensions={0} | all-to-all | bytes 262144 | tf_op jit(solution)/shard_map/all_to_all | solution.py:564
  54.2 3.7 %shard_map.105 = (f32[32,128]{1,0:T(8,128)S(1)}, f32[32,128]{1,0:T(8,128)S(1)}, f32[32,128]{1,0:T(8,128)S(1)}, s32[32,8,128]{2,1,0:T(8,128)S(1)}, s32[8,128]{1,0:T(8,128)S(1)}) custom-call(s32[1]{0:T(128)} %bitcast.base_ref, f32[128,2,128]{2,1,0:T(2,128)S(1)} %all_to_all.11.sums, f32[8,80,128]{2,1,0:T(8,128)S(1)} %all_to_all.10.rest_0_.rest_7_, ...), custom_call_target="tpu_custom_call" | custom-call | tf_op jit(solution)/shard_map/pallas_call | solution.py:493
  57.9 1.0 collective-permute-start.8
  58.8 1.5 %collective-permute-start.7 = (f32[32,128]{1,0:T(8,128)S(1)}, f32[32,128]{1,0:T(8,128)S(1)}, u32[]{:S(2)}, u32[]{:S(2)}) collective-permute-start(f32[32,128]{1,0:T(8,128)S(1)} %get-tuple-element.24.rest_0_), channel_id=1, source_target_pairs={{0,2},{1,3},{2,0},{3,1},{4,6},{5,7},{6,4},{7,5},{8,10},{9,11},{10,... | collective-permute-start | bytes 49160 | tf_op jit(solution)/shard_map/ppermute | solution.py:506
  60.3 0.0 collective-permute-start.6
  60.3 0.8 collective-permute-done.8.rest_3_
  61.1 0.6 collective-permute-done.7.rest_2_
  61.7 0.0 collective-permute-done.6.rest_1_
  61.7 2.1 %shard_map.106.rest_0_ = f32[32,128]{1,0:T(8,128)S(1)} custom-call(s32[1]{0:T(128)} %bitcast.base_ref, s32[8,128]{1,0:T(8,128)S(1)} %get-tuple-element.23.passes, f32[32,128]{1,0:T(8,128)S(1)} %get-tuple-element.24.rest_0_, f32[32,128]{1,0:T(8,128)S(1)} %collective-permute-done.6.rest_1_, f32[32,128]{1,0:T(8,128)S(1)} %collective-permute-done.7.rest_2_, ...), custom_call_target="tpu_custom_call" | custom-call | tf_op jit(solution)/shard_map/pallas_call | solution.py:493
  63.8 1.9 %collective-permute-start.11 = (f32[32,128]{1,0:T(8,128)S(1)}, f32[32,128]{1,0:T(8,128)S(1)}, u32[]{:S(2)}, u32[]{:S(2)}) collective-permute-start(f32[32,128]{1,0:T(8,128)S(1)} %shard_map.106.rest_0_), channel_id=1, source_target_pairs={{0,3},{1,2},{2,1},{3,0},{4,7},{5,6},{6,5},{7,4},{8,11},{9,10},{10,... | collective-permute-start | bytes 49160 | tf_op jit(solution)/shard_map/ppermute | solution.py:506
  65.7 1.7 %collective-permute-start.10 = (f32[32,128]{1,0:T(8,128)S(1)}, f32[32,128]{1,0:T(8,128)S(1)}, u32[]{:S(2)}, u32[]{:S(2)}) collective-permute-start(f32[32,128]{1,0:T(8,128)S(1)} %shard_map.106.rest_0_), channel_id=1, source_target_pairs={{0,2},{1,3},{2,0},{3,1},{4,6},{5,7},{6,4},{7,5},{8,10},{9,11},{10,... | collective-permute-start | bytes 49160 | tf_op jit(solution)/shard_map/ppermute | solution.py:506
  67.4 0.0 collective-permute-start.9
  67.4 1.4 %collective-permute-done.10.rest_2_ = f32[32,128]{1,0:T(8,128)S(1)} collective-permute-done((f32[32,128]{1,0:T(8,128)S(1)}, f32[32,128]{1,0:T(8,128)S(1)}, u32[]{:S(2)}, u32[]{:S(2)}) %collective-permute-start.10) | collective-permute-done | bytes 16416 | tf_op jit(solution)/shard_map/ppermute | solution.py:506
  68.8 2.1 %shard_map.107.rest_0_ = f32[32,128]{1,0:T(8,128)S(1)} custom-call(s32[1]{0:T(128)} %bitcast.base_ref, s32[8,128]{1,0:T(8,128)S(1)} %get-tuple-element.23.passes, f32[32,128]{1,0:T(8,128)S(1)} %shard_map.106.rest_0_, f32[32,128]{1,0:T(8,128)S(1)} %collective-permute-done.9.rest_1_, f32[32,128]{1,0:T(8,128)S(1)} %collective-permute-done.10.rest_2_, ...), custom_call_target="tpu_custom_call" | custom-call | tf_op jit(solution)/shard_map/pallas_call | solution.py:493
  70.9 0.0 copy-start.5
  70.9 1.2 %collective-permute-start.14 = (f32[32,128]{1,0:T(8,128)S(1)}, f32[32,128]{1,0:T(8,128)S(1)}, u32[]{:S(2)}, u32[]{:S(2)}) collective-permute-start(f32[32,128]{1,0:T(8,128)S(1)} %shard_map.107.rest_0_), channel_id=1, source_target_pairs={{0,3},{1,2},{2,1},{3,0},{4,7},{5,6},{6,5},{7,4},{8,11},{9,10},{10,... | collective-permute-start | bytes 49160 | tf_op jit(solution)/shard_map/ppermute | solution.py:506
  72.2 2.2 %collective-permute-start.13 = (f32[32,128]{1,0:T(8,128)S(1)}, f32[32,128]{1,0:T(8,128)S(1)}, u32[]{:S(2)}, u32[]{:S(2)}) collective-permute-start(f32[32,128]{1,0:T(8,128)S(1)} %shard_map.107.rest_0_), channel_id=1, source_target_pairs={{0,2},{1,3},{2,0},{3,1},{4,6},{5,7},{6,4},{7,5},{8,10},{9,11},{10,... | collective-permute-start | bytes 49160 | tf_op jit(solution)/shard_map/ppermute | solution.py:506
  74.3 1.4 %collective-permute-done.13.rest_2_ = f32[32,128]{1,0:T(8,128)S(1)} collective-permute-done((f32[32,128]{1,0:T(8,128)S(1)}, f32[32,128]{1,0:T(8,128)S(1)}, u32[]{:S(2)}, u32[]{:S(2)}) %collective-permute-start.13) | collective-permute-done | bytes 16416 | tf_op jit(solution)/shard_map/ppermute | solution.py:506
  75.7 0.0 collective-permute-done.12.rest_1_
  75.8 2.1 %shard_map.108.rest_0_ = f32[32,128]{1,0:T(8,128)S(1)} custom-call(s32[1]{0:T(128)} %bitcast.base_ref, s32[8,128]{1,0:T(8,128)S(1)} %get-tuple-element.23.passes, f32[32,128]{1,0:T(8,128)S(1)} %shard_map.107.rest_0_, f32[32,128]{1,0:T(8,128)S(1)} %collective-permute-done.12.rest_1_, f32[32,128]{1,0:T(8,128)S(1)} %collective-permute-done.13.rest_2_, ...), custom_call_target="tpu_custom_call" | custom-call | tf_op jit(solution)/shard_map/pallas_call | solution.py:493
  77.8 1.0 collective-permute-start.17
  78.9 2.2 %collective-permute-start.16 = (f32[32,128]{1,0:T(8,128)S(1)}, f32[32,128]{1,0:T(8,128)S(1)}, u32[]{:S(2)}, u32[]{:S(2)}) collective-permute-start(f32[32,128]{1,0:T(8,128)S(1)} %shard_map.108.rest_0_), channel_id=1, source_target_pairs={{0,2},{1,3},{2,0},{3,1},{4,6},{5,7},{6,4},{7,5},{8,10},{9,11},{10,... | collective-permute-start | bytes 49160 | tf_op jit(solution)/shard_map/ppermute | solution.py:506
  81.1 0.0 collective-permute-done.17.rest_3_
  81.1 1.4 %collective-permute-done.16.rest_2_ = f32[32,128]{1,0:T(8,128)S(1)} collective-permute-done((f32[32,128]{1,0:T(8,128)S(1)}, f32[32,128]{1,0:T(8,128)S(1)}, u32[]{:S(2)}, u32[]{:S(2)}) %collective-permute-start.16) | collective-permute-done | bytes 16416 | tf_op jit(solution)/shard_map/ppermute | solution.py:506
  82.5 0.0 collective-permute-done.15.rest_1_
  82.5 2.1 %shard_map.109.rest_0_ = f32[32,128]{1,0:T(8,128)S(1)} custom-call(s32[1]{0:T(128)} %bitcast.base_ref, s32[8,128]{1,0:T(8,128)S(1)} %get-tuple-element.23.passes, f32[32,128]{1,0:T(8,128)S(1)} %shard_map.108.rest_0_, f32[32,128]{1,0:T(8,128)S(1)} %collective-permute-done.15.rest_1_, f32[32,128]{1,0:T(8,128)S(1)} %collective-permute-done.16.rest_2_, ...), custom_call_target="tpu_custom_call" | custom-call | tf_op jit(solution)/shard_map/pallas_call | solution.py:493
  84.6 1.4 %collective-permute-start.20 = (f32[32,128]{1,0:T(8,128)S(1)}, f32[32,128]{1,0:T(8,128)S(1)}, u32[]{:S(2)}, u32[]{:S(2)}) collective-permute-start(f32[32,128]{1,0:T(8,128)S(1)} %shard_map.109.rest_0_), channel_id=1, source_target_pairs={{0,3},{1,2},{2,1},{3,0},{4,7},{5,6},{6,5},{7,4},{8,11},{9,10},{10,... | collective-permute-start | bytes 49160 | tf_op jit(solution)/shard_map/ppermute | solution.py:506
  86.0 2.2 %collective-permute-start.19 = (f32[32,128]{1,0:T(8,128)S(1)}, f32[32,128]{1,0:T(8,128)S(1)}, u32[]{:S(2)}, u32[]{:S(2)}) collective-permute-start(f32[32,128]{1,0:T(8,128)S(1)} %shard_map.109.rest_0_), channel_id=1, source_target_pairs={{0,2},{1,3},{2,0},{3,1},{4,6},{5,7},{6,4},{7,5},{8,10},{9,11},{10,... | collective-permute-start | bytes 49160 | tf_op jit(solution)/shard_map/ppermute | solution.py:506
  88.1 0.0 collective-permute-start.18
  88.1 5.8 %collective-permute-start.21 = (f32[3,256]{1,0:T(4,128)S(1)}, f32[3,256]{1,0:T(4,128)S(1)}, u32[]{:S(2)}, u32[]{:S(2)}) collective-permute-start(f32[3,256]{1,0:T(4,128)S(1)} %get-tuple-element.32), channel_id=1, source_target_pairs={{0,1},{1,2},{2,3},{3,4},{4,5},{5,6},{6,7},{7,8},{8,9},{9,10},{10,1... | collective-permute-start | bytes 9224 | tf_op jit(solution)/shard_map/ppermute | solution.py:518
  93.9 1.9 %collective-permute-start.22 = (f32[3,256]{1,0:T(4,128)S(1)}, f32[3,256]{1,0:T(4,128)S(1)}, u32[]{:S(2)}, u32[]{:S(2)}) collective-permute-start(f32[3,256]{1,0:T(4,128)S(1)} %get-tuple-element.33), channel_id=1, source_target_pairs={{1,0},{2,1},{3,2},{4,3},{5,4},{6,5},{7,6},{8,7},{9,8},{10,9},{11,1... | collective-permute-start | bytes 9224 | tf_op jit(solution)/shard_map/ppermute | solution.py:518
  95.9 0.0 collective-permute-done.21.rest_12_
  95.9 7.2 %collective-permute-done.22.rest_13_ = f32[3,256]{1,0:T(4,128)S(1)} collective-permute-done((f32[3,256]{1,0:T(4,128)S(1)}, f32[3,256]{1,0:T(4,128)S(1)}, u32[]{:S(2)}, u32[]{:S(2)}) %collective-permute-start.22) | collective-permute-done | bytes 3104 | tf_op jit(solution)/shard_map/ppermute | solution.py:518
  103.1 0.0 collective-permute-done.20.rest_3_
  103.1 0.0 collective-permute-done.19.rest_2_
  103.1 0.0 collective-permute-done.18.rest_1_
  103.1 2.7 %shard_map.110 = (f32[3,1024]{1,0:T(4,128)}, f32[3,32]{1,0:T(4,128)}) custom-call(s32[1]{0:T(128)} %bitcast.base_ref, f32[32,128]{1,0:T(8,128)S(1)} %shard_map.109.rest_0_, f32[32,128]{1,0:T(8,128)S(1)} %collective-permute-done.18.rest_1_, f32[32,128]{1,0:T(8,128)S(1)} %collective-permute-done.19.rest_2_, f32[32,128]{1,0:T(8,128)S(1)} %collective-permute-done.20.rest_3_, ...), custom_call_target="tpu_custom_call" | custom-call | tf_op jit(solution)/shard_map/pallas_call | solution.py:493
  (26 shorter events, 0.1 us)
Async XLA Ops:
  0.6 39.0 %copy-start = (f32[1024,27,3,3]{0,1,3,2:T(8,128)S(1)}, f32[1024,27,3,3]{0,1,3,2:T(8,128)}, u32[]{:S(2)}) copy-start(f32[1024,27,3,3]{0,1,3,2:T(8,128)} %param.12) | copy-start | bytes 2985988
  0.6 39.0 %copy-start.1 = (s32[1024,27]{0,1:T(8,128)S(1)}, s32[1024,27]{0,1:T(8,128)}, u32[]{:S(2)}) copy-start(s32[1024,27]{0,1:T(8,128)} %param.11) | copy-start | bytes 331780
  0.7 39.0 %copy-start.2 = (f32[1024,3]{0,1:T(4,128)S(1)}, f32[1024,3]{0,1:T(4,128)}, u32[]{:S(2)}) copy-start(f32[1024,3]{0,1:T(4,128)} %param.9) | copy-start | bytes 36868
  0.7 39.0 %copy-start.3 = (f32[1024,3]{0,1:T(4,128)S(1)}, f32[1024,3]{0,1:T(4,128)}, u32[]{:S(2)}) copy-start(f32[1024,3]{0,1:T(4,128)} %param.10) | copy-start | bytes 36868
  0.7 39.0 %copy-start.4 = (s32[1024]{0:T(1024)S(1)}, s32[1024]{0:T(1024)}, u32[]{:S(2)}) copy-start(s32[1024]{0:T(1024)} %param.13) | copy-start | bytes 12292
  0.7 39.0 %copy-start.6 = (f32[32,3]{0,1:T(4,128)S(1)}, f32[32,3]{0,1:T(4,128)}, u32[]{:S(2)}) copy-start(f32[32,3]{0,1:T(4,128)} %param.15) | copy-start | bytes 1156
  0.7 39.0 %copy-start.7 = (s32[32]{0:T(128)S(1)}, s32[32]{0:T(128)}, u32[]{:S(2)}) copy-start(s32[32]{0:T(128)} %param.14) | copy-start | bytes 388
  17.6 11.5 %collective-permute-start.3 = (f32[8,80,128]{2,1,0:T(8,128)S(1)}, f32[8,80,128]{2,1,0:T(8,128)S(1)}, u32[]{:S(2)}, u32[]{:S(2)}) collective-permute-start(f32[8,80,128]{2,1,0:T(8,128)S(1)} %all_to_all.10.rest_0_.rest_7_), channel_id=1, source_target_pairs={{0,32},{1,33},{2,34},{3,35},{4,36},{5,37},{6,38},{7,39},{8,40},{9,... | collective-permute-start | bytes 983048 | tf_op jit(solution)/shard_map/ppermute | solution.py:506
  17.6 11.6 %collective-permute-start.2 = (f32[8,80,128]{2,1,0:T(8,128)S(1)}, f32[8,80,128]{2,1,0:T(8,128)S(1)}, u32[]{:S(2)}, u32[]{:S(2)}) collective-permute-start(f32[8,80,128]{2,1,0:T(8,128)S(1)} %all_to_all.10.rest_0_.rest_7_), channel_id=1, source_target_pairs={{0,8},{1,9},{2,10},{3,11},{4,12},{5,13},{6,14},{7,15},{8,0},{9,1},... | collective-permute-start | bytes 983048 | tf_op jit(solution)/shard_map/ppermute | solution.py:506
  17.6 13.5 %collective-permute-start = (f32[288,256]{1,0:T(8,128)}, f32[288,256]{1,0:T(8,128)S(1)}, u32[]{:S(2)}, u32[]{:S(2)}) collective-permute-start(f32[288,256]{1,0:T(8,128)} %get-tuple-element.19), channel_id=1, source_target_pairs={{0,1},{1,2},{2,3},{3,4},{4,5},{5,6},{6,7},{7,8},{8,9},{9,10},{10,1... | collective-permute-start | bytes 884744 | tf_op jit(solution)/shard_map/ppermute | solution.py:518
  27.2 12.5 %collective-permute-start.1 = (f32[288,256]{1,0:T(8,128)}, f32[288,256]{1,0:T(8,128)S(1)}, u32[]{:S(2)}, u32[]{:S(2)}) collective-permute-start(f32[288,256]{1,0:T(8,128)} %get-tuple-element.20), channel_id=1, source_target_pairs={{1,0},{2,1},{3,2},{4,3},{5,4},{6,5},{7,6},{8,7},{9,8},{10,9},{11,1... | collective-permute-start | bytes 884744 | tf_op jit(solution)/shard_map/ppermute | solution.py:518
  29.2 25.0 %collective-permute-start.5 = (f32[4,80,128]{2,1,0:T(8,128)S(1)}, f32[4,80,128]{2,1,0:T(8,128)S(1)}, u32[]{:S(2)}, u32[]{:S(2)}) collective-permute-start(f32[4,80,128]{2,1,0:T(8,128)S(1)} %slice.9), channel_id=1, source_target_pairs={{0,8},{1,9},{2,10},{3,11},{4,12},{5,13},{6,14},{7,15},{8,0},{9,1},... | collective-permute-start | bytes 491528 | tf_op jit(solution)/shard_map/ppermute | solution.py:506
  29.9 24.3 %collective-permute-start.4 = (f32[4,80,128]{2,1,0:T(8,128)}, f32[4,80,128]{2,1,0:T(8,128)S(1)}, u32[]{:S(2)}, u32[]{:S(2)}) collective-permute-start(f32[4,80,128]{2,1,0:T(8,128)} %slice.8), channel_id=1, source_target_pairs={{0,32},{1,33},{2,34},{3,35},{4,36},{5,37},{6,38},{7,39},{8,40},{9,... | collective-permute-start | bytes 491528 | tf_op jit(solution)/shard_map/ppermute | solution.py:506
  57.9 3.2 %collective-permute-start.8 = (f32[32,128]{1,0:T(8,128)S(1)}, f32[32,128]{1,0:T(8,128)S(1)}, u32[]{:S(2)}, u32[]{:S(2)}) collective-permute-start(f32[32,128]{1,0:T(8,128)S(1)} %get-tuple-element.24.rest_0_), channel_id=1, source_target_pairs={{0,3},{1,2},{2,1},{3,0},{4,7},{5,6},{6,5},{7,4},{8,11},{9,10},{10,... | collective-permute-start | bytes 49160 | tf_op jit(solution)/shard_map/ppermute | solution.py:506
  58.8 2.9 %collective-permute-start.7 = (f32[32,128]{1,0:T(8,128)S(1)}, f32[32,128]{1,0:T(8,128)S(1)}, u32[]{:S(2)}, u32[]{:S(2)}) collective-permute-start(f32[32,128]{1,0:T(8,128)S(1)} %get-tuple-element.24.rest_0_), channel_id=1, source_target_pairs={{0,2},{1,3},{2,0},{3,1},{4,6},{5,7},{6,4},{7,5},{8,10},{9,11},{10,... | collective-permute-start | bytes 49160 | tf_op jit(solution)/shard_map/ppermute | solution.py:506
  60.3 1.4 %collective-permute-start.6 = (f32[32,128]{1,0:T(8,128)S(1)}, f32[32,128]{1,0:T(8,128)S(1)}, u32[]{:S(2)}, u32[]{:S(2)}) collective-permute-start(f32[32,128]{1,0:T(8,128)S(1)} %get-tuple-element.24.rest_0_), channel_id=1, source_target_pairs={{0,1},{1,0},{2,3},{3,2},{4,5},{5,4},{6,7},{7,6},{8,9},{9,8},{10,11... | collective-permute-start | bytes 49160 | tf_op jit(solution)/shard_map/ppermute | solution.py:506
  63.8 3.6 %collective-permute-start.11 = (f32[32,128]{1,0:T(8,128)S(1)}, f32[32,128]{1,0:T(8,128)S(1)}, u32[]{:S(2)}, u32[]{:S(2)}) collective-permute-start(f32[32,128]{1,0:T(8,128)S(1)} %shard_map.106.rest_0_), channel_id=1, source_target_pairs={{0,3},{1,2},{2,1},{3,0},{4,7},{5,6},{6,5},{7,4},{8,11},{9,10},{10,... | collective-permute-start | bytes 49160 | tf_op jit(solution)/shard_map/ppermute | solution.py:506
  65.7 3.1 %collective-permute-start.10 = (f32[32,128]{1,0:T(8,128)S(1)}, f32[32,128]{1,0:T(8,128)S(1)}, u32[]{:S(2)}, u32[]{:S(2)}) collective-permute-start(f32[32,128]{1,0:T(8,128)S(1)} %shard_map.106.rest_0_), channel_id=1, source_target_pairs={{0,2},{1,3},{2,0},{3,1},{4,6},{5,7},{6,4},{7,5},{8,10},{9,11},{10,... | collective-permute-start | bytes 49160 | tf_op jit(solution)/shard_map/ppermute | solution.py:506
  67.4 1.4 %collective-permute-start.9 = (f32[32,128]{1,0:T(8,128)S(1)}, f32[32,128]{1,0:T(8,128)S(1)}, u32[]{:S(2)}, u32[]{:S(2)}) collective-permute-start(f32[32,128]{1,0:T(8,128)S(1)} %shard_map.106.rest_0_), channel_id=1, source_target_pairs={{0,1},{1,0},{2,3},{3,2},{4,5},{5,4},{6,7},{7,6},{8,9},{9,8},{10,11... | collective-permute-start | bytes 49160 | tf_op jit(solution)/shard_map/ppermute | solution.py:506
  70.9 32.2 %copy-start.5 = (f32[8,128]{1,0:T(8,128)S(1)}, f32[8,128]{1,0:T(8,128)}, u32[]{:S(2)}) copy-start(f32[8,128]{1,0:T(8,128)} %get-tuple-element.31.rest_9_) | copy-start | bytes 12292
  70.9 3.4 %collective-permute-start.14 = (f32[32,128]{1,0:T(8,128)S(1)}, f32[32,128]{1,0:T(8,128)S(1)}, u32[]{:S(2)}, u32[]{:S(2)}) collective-permute-start(f32[32,128]{1,0:T(8,128)S(1)} %shard_map.107.rest_0_), channel_id=1, source_target_pairs={{0,3},{1,2},{2,1},{3,0},{4,7},{5,6},{6,5},{7,4},{8,11},{9,10},{10,... | collective-permute-start | bytes 49160 | tf_op jit(solution)/shard_map/ppermute | solution.py:506
  72.2 3.6 %collective-permute-start.13 = (f32[32,128]{1,0:T(8,128)S(1)}, f32[32,128]{1,0:T(8,128)S(1)}, u32[]{:S(2)}, u32[]{:S(2)}) collective-permute-start(f32[32,128]{1,0:T(8,128)S(1)} %shard_map.107.rest_0_), channel_id=1, source_target_pairs={{0,2},{1,3},{2,0},{3,1},{4,6},{5,7},{6,4},{7,5},{8,10},{9,11},{10,... | collective-permute-start | bytes 49160 | tf_op jit(solution)/shard_map/ppermute | solution.py:506
  74.3 1.4 %collective-permute-start.12 = (f32[32,128]{1,0:T(8,128)S(1)}, f32[32,128]{1,0:T(8,128)S(1)}, u32[]{:S(2)}, u32[]{:S(2)}) collective-permute-start(f32[32,128]{1,0:T(8,128)S(1)} %shard_map.107.rest_0_), channel_id=1, source_target_pairs={{0,1},{1,0},{2,3},{3,2},{4,5},{5,4},{6,7},{7,6},{8,9},{9,8},{10,11... | collective-permute-start | bytes 49160 | tf_op jit(solution)/shard_map/ppermute | solution.py:506
  77.8 3.2 %collective-permute-start.17 = (f32[32,128]{1,0:T(8,128)S(1)}, f32[32,128]{1,0:T(8,128)S(1)}, u32[]{:S(2)}, u32[]{:S(2)}) collective-permute-start(f32[32,128]{1,0:T(8,128)S(1)} %shard_map.108.rest_0_), channel_id=1, source_target_pairs={{0,3},{1,2},{2,1},{3,0},{4,7},{5,6},{6,5},{7,4},{8,11},{9,10},{10,... | collective-permute-start | bytes 49160 | tf_op jit(solution)/shard_map/ppermute | solution.py:506
  78.9 3.6 %collective-permute-start.16 = (f32[32,128]{1,0:T(8,128)S(1)}, f32[32,128]{1,0:T(8,128)S(1)}, u32[]{:S(2)}, u32[]{:S(2)}) collective-permute-start(f32[32,128]{1,0:T(8,128)S(1)} %shard_map.108.rest_0_), channel_id=1, source_target_pairs={{0,2},{1,3},{2,0},{3,1},{4,6},{5,7},{6,4},{7,5},{8,10},{9,11},{10,... | collective-permute-start | bytes 49160 | tf_op jit(solution)/shard_map/ppermute | solution.py:506
  81.0 1.4 %collective-permute-start.15 = (f32[32,128]{1,0:T(8,128)S(1)}, f32[32,128]{1,0:T(8,128)S(1)}, u32[]{:S(2)}, u32[]{:S(2)}) collective-permute-start(f32[32,128]{1,0:T(8,128)S(1)} %shard_map.108.rest_0_), channel_id=1, source_target_pairs={{0,1},{1,0},{2,3},{3,2},{4,5},{5,4},{6,7},{7,6},{8,9},{9,8},{10,11... | collective-permute-start | bytes 49160 | tf_op jit(solution)/shard_map/ppermute | solution.py:506
  84.6 18.5 %collective-permute-start.20 = (f32[32,128]{1,0:T(8,128)S(1)}, f32[32,128]{1,0:T(8,128)S(1)}, u32[]{:S(2)}, u32[]{:S(2)}) collective-permute-start(f32[32,128]{1,0:T(8,128)S(1)} %shard_map.109.rest_0_), channel_id=1, source_target_pairs={{0,3},{1,2},{2,1},{3,0},{4,7},{5,6},{6,5},{7,4},{8,11},{9,10},{10,... | collective-permute-start | bytes 49160 | tf_op jit(solution)/shard_map/ppermute | solution.py:506
  86.0 17.1 %collective-permute-start.19 = (f32[32,128]{1,0:T(8,128)S(1)}, f32[32,128]{1,0:T(8,128)S(1)}, u32[]{:S(2)}, u32[]{:S(2)}) collective-permute-start(f32[32,128]{1,0:T(8,128)S(1)} %shard_map.109.rest_0_), channel_id=1, source_target_pairs={{0,2},{1,3},{2,0},{3,1},{4,6},{5,7},{6,4},{7,5},{8,10},{9,11},{10,... | collective-permute-start | bytes 49160 | tf_op jit(solution)/shard_map/ppermute | solution.py:506
  88.1 15.0 %collective-permute-start.18 = (f32[32,128]{1,0:T(8,128)S(1)}, f32[32,128]{1,0:T(8,128)S(1)}, u32[]{:S(2)}, u32[]{:S(2)}) collective-permute-start(f32[32,128]{1,0:T(8,128)S(1)} %shard_map.109.rest_0_), channel_id=1, source_target_pairs={{0,1},{1,0},{2,3},{3,2},{4,5},{5,4},{6,7},{7,6},{8,9},{9,8},{10,11... | collective-permute-start | bytes 49160 | tf_op jit(solution)/shard_map/ppermute | solution.py:506
  88.1 7.7 %collective-permute-start.21 = (f32[3,256]{1,0:T(4,128)S(1)}, f32[3,256]{1,0:T(4,128)S(1)}, u32[]{:S(2)}, u32[]{:S(2)}) collective-permute-start(f32[3,256]{1,0:T(4,128)S(1)} %get-tuple-element.32), channel_id=1, source_target_pairs={{0,1},{1,2},{2,3},{3,4},{4,5},{5,6},{6,7},{7,8},{8,9},{9,10},{10,1... | collective-permute-start | bytes 9224 | tf_op jit(solution)/shard_map/ppermute | solution.py:518
  93.9 9.1 %collective-permute-start.22 = (f32[3,256]{1,0:T(4,128)S(1)}, f32[3,256]{1,0:T(4,128)S(1)}, u32[]{:S(2)}, u32[]{:S(2)}) collective-permute-start(f32[3,256]{1,0:T(4,128)S(1)} %get-tuple-element.33), channel_id=1, source_target_pairs={{1,0},{2,1},{3,2},{4,3},{5,4},{6,5},{7,6},{8,7},{9,8},{10,9},{11,1... | collective-permute-start | bytes 9224 | tf_op jit(solution)/shard_map/ppermute | solution.py:518

commit v2 on v0

--- a/solution.py
+++ b/solution.py
@@ -544,6 +544,27 @@
     data = lax.all_to_all(
         dsend, DOM, 0, 0, axis_index_groups=row_groups(), tiled=True
     )
+    data = (data, partner(data, 8), partner(data, 32), partner(data, 40))
+    vmem, far = pl.BlockSpec(memory_space=pltpu.VMEM), pl.BlockSpec(memory_space=pltpu.HBM)
+    up, down, node_row, dsend = pl.pallas_call(
+        pack_kernel,
+        name="pack",
+        in_specs=[far] * 8,
+        out_specs=[vmem] * 4,
+        out_shape=[jax.ShapeDtypeStruct(o, f32)
+            for o in ((P_ALL, HALO), (P_ALL, HALO), (8, LANES), (NEAR, 80, LANES))],
+        scratch_shapes=[
+            pltpu.VMEM((3, ROWS), f32), pltpu.VMEM((3, ROWS), f32),
+            pltpu.VMEM((2, SLOTS, HALO), i32), pltpu.VMEM((2, 3, 3, SLOTS, HALO), f32),
+            pltpu.VMEM((8, LANES), i32), pltpu.VMEM((1, 32), i32),
+            pltpu.VMEM((32, SLOTS), i32), pltpu.VMEM((3, 3, 32, SLOTS), f32),
+            pltpu.SemaphoreType.DMA((10,)),
+        ],
+        compiler_params=pltpu.CompilerParams(vmem_limit_bytes=60 * 2**20),
+    )(rhs, dia, col, blk, agg, owner, coarse_columns, cblk)
+    data = lax.all_to_all(
+        dsend, DOM, 0, 0, axis_index_groups=row_groups(), tiled=True
+    )
     along_z, along_y = partner(data, 8), partner(data, 32)
     data = (data, along_z, along_y, partner(along_z, 32))
     before, after = shifts(up, down)

time: 105 us -> 105 us (level)
  no operation moved by 1% of the time
where the time goes in v2:
time: 105 us
  starting transfers between devices  33.7 us (32%)
  blocking collectives  29.3 us (28%)
  waiting for transfers between devices  22 us (21%)
  Pallas kernels  19.2 us (18%)
    ppermute x18, starting transfers between devices, partner(): lax.ppermute(value, DOM, [(i, i ^ bits) for i in range(lax.axis_size(DOM))])  17.6 us
    pallas_call x7, Pallas kernels, call(): pl.pallas_call(kernel, in_specs=[smem] * scalars + [vmem] * (len(args) -...  16.8 us
    ppermute x4, waiting for transfers between devices, shifts(): return (lax.ppermute(up, DOM, forward), lax.ppermute(down, DOM, backward))  16.3 us
    ppermute x4, starting transfers between devices, shifts(): return (lax.ppermute(up, DOM, forward), lax.ppermute(down, DOM, backward))  16.1 us
    all_to_all x1, blocking collectives, cycle(): sums = lax.all_to_all(send, DOM, 0, 0, tiled=True)  14.9 us
    all_to_all x1, blocking collectives, cycle(): lax.all_to_all(dsend, DOM, 0, 0, axis_index_groups=row_groups(), tiled=True)  14.5 us
    ppermute x18, waiting for transfers between devices, partner(): lax.ppermute(value, DOM, [(i, i ^ bits) for i in range(lax.axis_size(DOM))])  5.68 us
    pallas_call x1, Pallas kernels, cycle(): pl.pallas_call(pack_kernel, name='pack', in_specs=[far] * 8, out_specs=[v...  2.47 us
  transfers between devices with their start and end apart: 22, of which 8 were waited for; matrix products, arithmetic and copies ran while one was open for 0% of the time, Pallas kernels for 2%

profile of v2, /device:TPU:103, one launch (start us, length us, event | category | flops | bytes accessed | tf_op | source)
XLA Modules:
  0.0 105.1 jit_solution(12434451521522358879)
XLA Ops:
  0.7 2.5 %pack.1 = (f32[288,256]{1,0:T(8,128)}, f32[288,256]{1,0:T(8,128)}, f32[8,128]{1,0:T(8,128)}, f32[8,80,128]{2,1,0:T(8,128)}) custom-call(f32[3,1024]{1,0:T(4,128)} %bitcast.17, f32[3,1024]{1,0:T(4,128)} %bitcast.19, s32[27,1024]{1,0:T(8,128)} %bitcast.14, f32[3,3,27,1024]{3,2,1,0:T(8,128)} %bitcast.11, s32[8,128]{1,0:T(8,128)} %bitcast.21, s32[1,32]{1,0:T(1,128)} %bitcast.24, ...), custom_call_target="tpu_custom_call" | custom-call | tf_op jit(solution)/shard_map/pack/pallas_call | solution.py:549
  3.2 14.5 %all_to_all.10.rest_0_.rest_7_ = f32[8,80,128]{2,1,0:T(8,128)S(1)} all-to-all(f32[8,80,128]{2,1,0:T(8,128)} %get-tuple-element.22), channel_id=1, replica_groups={{0,6,24,30,96,102,120,126},{1,7,25,31,97,103,121,127},{2,4,26,28,98,100..., dimensions={0} | all-to-all | bytes 655360 | tf_op jit(solution)/shard_map/all_to_all | solution.py:565
  17.6 0.0 collective-permute-start.2
  17.6 6.5 %collective-permute-start = (f32[288,256]{1,0:T(8,128)}, f32[288,256]{1,0:T(8,128)S(1)}, u32[]{:S(2)}, u32[]{:S(2)}) collective-permute-start(f32[288,256]{1,0:T(8,128)} %get-tuple-element.19), channel_id=1, source_target_pairs={{0,1},{1,2},{2,3},{3,4},{4,5},{5,6},{6,7},{7,8},{8,9},{9,10},{10,1... | collective-permute-start | bytes 884744 | tf_op jit(solution)/shard_map/ppermute | solution.py:513
  24.1 1.9 %collective-permute-start.1 = (f32[288,256]{1,0:T(8,128)}, f32[288,256]{1,0:T(8,128)S(1)}, u32[]{:S(2)}, u32[]{:S(2)}) collective-permute-start(f32[288,256]{1,0:T(8,128)} %get-tuple-element.20), channel_id=1, source_target_pairs={{1,0},{2,1},{3,2},{4,3},{5,4},{6,5},{7,6},{8,7},{9,8},{10,9},{11,1... | collective-permute-start | bytes 884744 | tf_op jit(solution)/shard_map/ppermute | solution.py:513
  26.0 0.4 collective-permute-start.3
  26.4 0.0 collective-permute-done.2.rest_1_.rest_8_
  26.4 1.2 %collective-permute-start.4 = (f32[8,80,128]{2,1,0:T(8,128)S(1)}, f32[8,80,128]{2,1,0:T(8,128)S(1)}, u32[]{:S(2)}, u32[]{:S(2)}) collective-permute-start(f32[8,80,128]{2,1,0:T(8,128)S(1)} %collective-permute-done.2.rest_1_.rest_8_), channel_id=1, source_target_pairs={{0,32},{1,33},{2,34},{3,35},{4,36},{5,37},{6,38},{7,39},{8,40},{9,... | collective-permute-start | bytes 983048 | tf_op jit(solution)/shard_map/ppermute | solution.py:501
  27.6 0.5 collective-permute-done.before.rest_10_
  28.1 8.6 %collective-permute-done.1.after.rest_11_ = f32[288,256]{1,0:T(8,128)S(1)} collective-permute-done((f32[288,256]{1,0:T(8,128)}, f32[288,256]{1,0:T(8,128)S(1)}, u32[]{:S(2)}, u32[]{:S(2)}) %collective-permute-start.1) | collective-permute-done | bytes 294944 | tf_op jit(solution)/shard_map/ppermute | solution.py:513
  36.7 2.1 %shard_map.104 = (f32[128,2,128]{2,1,0:T(2,128)S(1)}, f32[3,2048]{1,0:T(4,128)S(1)}, f32[3,2048]{1,0:T(4,128)S(1)}, f32[3,2048]{1,0:T(4,128)S(1)}, f32[3,256]{1,0:T(4,128)S(1)}, /*index=5*/f32[3,256]{1,0:T(4,128)S(1)}) custom-call(s32[1]{0:T(128)} %bitcast.base_ref, f32[3,1024]{1,0:T(4,128)S(1)} %bitcast.18, f32[3,1024]{1,0:T(4,128)S(1)} %bitcast.20, ...), custom_call_target="tpu_custom_call" | custom-call | tf_op jit(solution)/shard_map/pallas_call | solution.py:488
  38.9 14.9 %all_to_all.11.sums = f32[128,2,128]{2,1,0:T(2,128)S(1)} all-to-all(f32[128,2,128]{2,1,0:T(2,128)S(1)} %get-tuple-element.21), channel_id=1, replica_groups=mesh['dom'=128] {'dom'}, dimensions={0} | all-to-all | bytes 262144 | tf_op jit(solution)/shard_map/all_to_all | solution.py:579
  53.7 0.0 collective-permute-done.3.rest_2_.rest_9_
  53.7 0.0 collective-permute-done.4.rest_3_.rest_10_
  53.7 3.7 %shard_map.105 = (f32[32,128]{1,0:T(8,128)S(1)}, f32[32,128]{1,0:T(8,128)S(1)}, f32[32,128]{1,0:T(8,128)S(1)}, s32[32,8,128]{2,1,0:T(8,128)S(1)}, s32[8,128]{1,0:T(8,128)S(1)}) custom-call(s32[1]{0:T(128)} %bitcast.base_ref, f32[128,2,128]{2,1,0:T(2,128)S(1)} %all_to_all.11.sums, f32[8,80,128]{2,1,0:T(8,128)S(1)} %all_to_all.10.rest_0_.rest_7_, ...), custom_call_target="tpu_custom_call" | custom-call | tf_op jit(solution)/shard_map/pallas_call | solution.py:488
  57.4 1.0 collective-permute-start.7
  58.4 1.5 %collective-permute-start.6 = (f32[32,128]{1,0:T(8,128)S(1)}, f32[32,128]{1,0:T(8,128)S(1)}, u32[]{:S(2)}, u32[]{:S(2)}) collective-permute-start(f32[32,128]{1,0:T(8,128)S(1)} %get-tuple-element.24.rest_0_), channel_id=1, source_target_pairs={{0,2},{1,3},{2,0},{3,1},{4,6},{5,7},{6,4},{7,5},{8,10},{9,11},{10,... | collective-permute-start | bytes 49160 | tf_op jit(solution)/shard_map/ppermute | solution.py:501
  59.8 0.0 collective-permute-start.5
  59.8 0.8 collective-permute-done.7.rest_3_
  60.6 0.6 collective-permute-done.6.rest_2_
  61.3 2.1 %shard_map.106.rest_0_ = f32[32,128]{1,0:T(8,128)S(1)} custom-call(s32[1]{0:T(128)} %bitcast.base_ref, s32[8,128]{1,0:T(8,128)S(1)} %get-tuple-element.23.passes, f32[32,128]{1,0:T(8,128)S(1)} %get-tuple-element.24.rest_0_, f32[32,128]{1,0:T(8,128)S(1)} %collective-permute-done.5.rest_1_, f32[32,128]{1,0:T(8,128)S(1)} %collective-permute-done.6.rest_2_, ...), custom_call_target="tpu_custom_call" | custom-call | tf_op jit(solution)/shard_map/pallas_call | solution.py:488
  63.3 1.9 %collective-permute-start.10 = (f32[32,128]{1,0:T(8,128)S(1)}, f32[32,128]{1,0:T(8,128)S(1)}, u32[]{:S(2)}, u32[]{:S(2)}) collective-permute-start(f32[32,128]{1,0:T(8,128)S(1)} %shard_map.106.rest_0_), channel_id=1, source_target_pairs={{0,3},{1,2},{2,1},{3,0},{4,7},{5,6},{6,5},{7,4},{8,11},{9,10},{10,... | collective-permute-start | bytes 49160 | tf_op jit(solution)/shard_map/ppermute | solution.py:501
  65.3 1.7 %collective-permute-start.9 = (f32[32,128]{1,0:T(8,128)S(1)}, f32[32,128]{1,0:T(8,128)S(1)}, u32[]{:S(2)}, u32[]{:S(2)}) collective-permute-start(f32[32,128]{1,0:T(8,128)S(1)} %shard_map.106.rest_0_), channel_id=1, source_target_pairs={{0,2},{1,3},{2,0},{3,1},{4,6},{5,7},{6,4},{7,5},{8,10},{9,11},{10,... | collective-permute-start | bytes 49160 | tf_op jit(solution)/shard_map/ppermute | solution.py:501
  67.0 1.4 %collective-permute-done.9.rest_2_ = f32[32,128]{1,0:T(8,128)S(1)} collective-permute-done((f32[32,128]{1,0:T(8,128)S(1)}, f32[32,128]{1,0:T(8,128)S(1)}, u32[]{:S(2)}, u32[]{:S(2)}) %collective-permute-start.9) | collective-permute-done | bytes 16416 | tf_op jit(solution)/shard_map/ppermute | solution.py:501
  68.4 0.0 collective-permute-done.8.rest_1_
  68.4 2.1 %shard_map.107.rest_0_ = f32[32,128]{1,0:T(8,128)S(1)} custom-call(s32[1]{0:T(128)} %bitcast.base_ref, s32[8,128]{1,0:T(8,128)S(1)} %get-tuple-element.23.passes, f32[32,128]{1,0:T(8,128)S(1)} %shard_map.106.rest_0_, f32[32,128]{1,0:T(8,128)S(1)} %collective-permute-done.8.rest_1_, f32[32,128]{1,0:T(8,128)S(1)} %collective-permute-done.9.rest_2_, ...), custom_call_target="tpu_custom_call" | custom-call | tf_op jit(solution)/shard_map/pallas_call | solution.py:488
  70.5 0.0 copy-start.5
  70.5 1.2 %collective-permute-start.13 = (f32[32,128]{1,0:T(8,128)S(1)}, f32[32,128]{1,0:T(8,128)S(1)}, u32[]{:S(2)}, u32[]{:S(2)}) collective-permute-start(f32[32,128]{1,0:T(8,128)S(1)} %shard_map.107.rest_0_), channel_id=1, source_target_pairs={{0,3},{1,2},{2,1},{3,0},{4,7},{5,6},{6,5},{7,4},{8,11},{9,10},{10,... | collective-permute-start | bytes 49160 | tf_op jit(solution)/shard_map/ppermute | solution.py:501
  71.7 2.2 %collective-permute-start.12 = (f32[32,128]{1,0:T(8,128)S(1)}, f32[32,128]{1,0:T(8,128)S(1)}, u32[]{:S(2)}, u32[]{:S(2)}) collective-permute-start(f32[32,128]{1,0:T(8,128)S(1)} %shard_map.107.rest_0_), channel_id=1, source_target_pairs={{0,2},{1,3},{2,0},{3,1},{4,6},{5,7},{6,4},{7,5},{8,10},{9,11},{10,... | collective-permute-start | bytes 49160 | tf_op jit(solution)/shard_map/ppermute | solution.py:501
  73.9 1.4 %collective-permute-done.12.rest_2_ = f32[32,128]{1,0:T(8,128)S(1)} collective-permute-done((f32[32,128]{1,0:T(8,128)S(1)}, f32[32,128]{1,0:T(8,128)S(1)}, u32[]{:S(2)}, u32[]{:S(2)}) %collective-permute-start.12) | collective-permute-done | bytes 16416 | tf_op jit(solution)/shard_map/ppermute | solution.py:501
  75.3 0.0 collective-permute-done.11.rest_1_
  75.3 2.1 %shard_map.108.rest_0_ = f32[32,128]{1,0:T(8,128)S(1)} custom-call(s32[1]{0:T(128)} %bitcast.base_ref, s32[8,128]{1,0:T(8,128)S(1)} %get-tuple-element.23.passes, f32[32,128]{1,0:T(8,128)S(1)} %shard_map.107.rest_0_, f32[32,128]{1,0:T(8,128)S(1)} %collective-permute-done.11.rest_1_, f32[32,128]{1,0:T(8,128)S(1)} %collective-permute-done.12.rest_2_, ...), custom_call_target="tpu_custom_call" | custom-call | tf_op jit(solution)/shard_map/pallas_call | solution.py:488
  77.4 1.0 collective-permute-start.16
  78.4 2.2 %collective-permute-start.15 = (f32[32,128]{1,0:T(8,128)S(1)}, f32[32,128]{1,0:T(8,128)S(1)}, u32[]{:S(2)}, u32[]{:S(2)}) collective-permute-start(f32[32,128]{1,0:T(8,128)S(1)} %shard_map.108.rest_0_), channel_id=1, source_target_pairs={{0,2},{1,3},{2,0},{3,1},{4,6},{5,7},{6,4},{7,5},{8,10},{9,11},{10,... | collective-permute-start | bytes 49160 | tf_op jit(solution)/shard_map/ppermute | solution.py:501
  80.6 0.0 collective-permute-start.14
  80.6 0.0 collective-permute-done.16.rest_3_
  80.6 1.4 %collective-permute-done.15.rest_2_ = f32[32,128]{1,0:T(8,128)S(1)} collective-permute-done((f32[32,128]{1,0:T(8,128)S(1)}, f32[32,128]{1,0:T(8,128)S(1)}, u32[]{:S(2)}, u32[]{:S(2)}) %collective-permute-start.15) | collective-permute-done | bytes 16416 | tf_op jit(solution)/shard_map/ppermute | solution.py:501
  82.0 0.0 collective-permute-done.14.rest_1_
  82.0 2.1 %shard_map.109.rest_0_ = f32[32,128]{1,0:T(8,128)S(1)} custom-call(s32[1]{0:T(128)} %bitcast.base_ref, s32[8,128]{1,0:T(8,128)S(1)} %get-tuple-element.23.passes, f32[32,128]{1,0:T(8,128)S(1)} %shard_map.108.rest_0_, f32[32,128]{1,0:T(8,128)S(1)} %collective-permute-done.14.rest_1_, f32[32,128]{1,0:T(8,128)S(1)} %collective-permute-done.15.rest_2_, ...), custom_call_target="tpu_custom_call" | custom-call | tf_op jit(solution)/shard_map/pallas_call | solution.py:488
  84.1 1.2 %collective-permute-start.19 = (f32[32,128]{1,0:T(8,128)S(1)}, f32[32,128]{1,0:T(8,128)S(1)}, u32[]{:S(2)}, u32[]{:S(2)}) collective-permute-start(f32[32,128]{1,0:T(8,128)S(1)} %shard_map.109.rest_0_), channel_id=1, source_target_pairs={{0,3},{1,2},{2,1},{3,0},{4,7},{5,6},{6,5},{7,4},{8,11},{9,10},{10,... | collective-permute-start | bytes 49160 | tf_op jit(solution)/shard_map/ppermute | solution.py:501
  85.3 2.2 %collective-permute-start.18 = (f32[32,128]{1,0:T(8,128)S(1)}, f32[32,128]{1,0:T(8,128)S(1)}, u32[]{:S(2)}, u32[]{:S(2)}) collective-permute-start(f32[32,128]{1,0:T(8,128)S(1)} %shard_map.109.rest_0_), channel_id=1, source_target_pairs={{0,2},{1,3},{2,0},{3,1},{4,6},{5,7},{6,4},{7,5},{8,10},{9,11},{10,... | collective-permute-start | bytes 49160 | tf_op jit(solution)/shard_map/ppermute | solution.py:501
  87.5 0.0 collective-permute-start.17
  87.5 5.8 %collective-permute-start.20 = (f32[3,256]{1,0:T(4,128)S(1)}, f32[3,256]{1,0:T(4,128)S(1)}, u32[]{:S(2)}, u32[]{:S(2)}) collective-permute-start(f32[3,256]{1,0:T(4,128)S(1)} %get-tuple-element.32), channel_id=1, source_target_pairs={{0,1},{1,2},{2,3},{3,4},{4,5},{5,6},{6,7},{7,8},{8,9},{9,10},{10,1... | collective-permute-start | bytes 9224 | tf_op jit(solution)/shard_map/ppermute | solution.py:513
  93.3 1.9 %collective-permute-start.21 = (f32[3,256]{1,0:T(4,128)S(1)}, f32[3,256]{1,0:T(4,128)S(1)}, u32[]{:S(2)}, u32[]{:S(2)}) collective-permute-start(f32[3,256]{1,0:T(4,128)S(1)} %get-tuple-element.33), channel_id=1, source_target_pairs={{1,0},{2,1},{3,2},{4,3},{5,4},{6,5},{7,6},{8,7},{9,8},{10,9},{11,1... | collective-permute-start | bytes 9224 | tf_op jit(solution)/shard_map/ppermute | solution.py:513
  95.2 7.2 %collective-permute-done.21.rest_13_ = f32[3,256]{1,0:T(4,128)S(1)} collective-permute-done((f32[3,256]{1,0:T(4,128)S(1)}, f32[3,256]{1,0:T(4,128)S(1)}, u32[]{:S(2)}, u32[]{:S(2)}) %collective-permute-start.21) | collective-permute-done | bytes 3104 | tf_op jit(solution)/shard_map/ppermute | solution.py:513
  102.4 0.0 collective-permute-done.19.rest_3_
  102.4 0.0 collective-permute-done.18.rest_2_
  102.5 2.7 %shard_map.110 = (f32[3,1024]{1,0:T(4,128)}, f32[3,32]{1,0:T(4,128)}) custom-call(s32[1]{0:T(128)} %bitcast.base_ref, f32[32,128]{1,0:T(8,128)S(1)} %shard_map.109.rest_0_, f32[32,128]{1,0:T(8,128)S(1)} %collective-permute-done.17.rest_1_, f32[32,128]{1,0:T(8,128)S(1)} %collective-permute-done.18.rest_2_, f32[32,128]{1,0:T(8,128)S(1)} %collective-permute-done.19.rest_3_, ...), custom_call_target="tpu_custom_call" | custom-call | tf_op jit(solution)/shard_map/pallas_call | solution.py:488
  (22 shorter events, 0.1 us)
Async XLA Ops:
  0.6 36.1 %copy-start.7 = (s32[32]{0:T(128)S(1)}, s32[32]{0:T(128)}, u32[]{:S(2)}) copy-start(s32[32]{0:T(128)} %param.14) | copy-start | bytes 388
  0.6 36.0 %copy-start.4 = (s32[1024]{0:T(1024)S(1)}, s32[1024]{0:T(1024)}, u32[]{:S(2)}) copy-start(s32[1024]{0:T(1024)} %param.13) | copy-start | bytes 12292
  0.7 36.0 %copy-start = (f32[1024,27,3,3]{0,1,3,2:T(8,128)S(1)}, f32[1024,27,3,3]{0,1,3,2:T(8,128)}, u32[]{:S(2)}) copy-start(f32[1024,27,3,3]{0,1,3,2:T(8,128)} %param.12) | copy-start | bytes 2985988
  0.7 36.0 %copy-start.1 = (s32[1024,27]{0,1:T(8,128)S(1)}, s32[1024,27]{0,1:T(8,128)}, u32[]{:S(2)}) copy-start(s32[1024,27]{0,1:T(8,128)} %param.11) | copy-start | bytes 331780
  0.7 36.0 %copy-start.3 = (f32[1024,3]{0,1:T(4,128)S(1)}, f32[1024,3]{0,1:T(4,128)}, u32[]{:S(2)}) copy-start(f32[1024,3]{0,1:T(4,128)} %param.10) | copy-start | bytes 36868
  0.7 36.0 %copy-start.2 = (f32[1024,3]{0,1:T(4,128)S(1)}, f32[1024,3]{0,1:T(4,128)}, u32[]{:S(2)}) copy-start(f32[1024,3]{0,1:T(4,128)} %param.9) | copy-start | bytes 36868
  0.7 36.0 %copy-start.6 = (f32[32,3]{0,1:T(4,128)S(1)}, f32[32,3]{0,1:T(4,128)}, u32[]{:S(2)}) copy-start(f32[32,3]{0,1:T(4,128)} %param.15) | copy-start | bytes 1156
  17.6 8.8 %collective-permute-start.2 = (f32[8,80,128]{2,1,0:T(8,128)S(1)}, f32[8,80,128]{2,1,0:T(8,128)S(1)}, u32[]{:S(2)}, u32[]{:S(2)}) collective-permute-start(f32[8,80,128]{2,1,0:T(8,128)S(1)} %all_to_all.10.rest_0_.rest_7_), channel_id=1, source_target_pairs={{0,8},{1,9},{2,10},{3,11},{4,12},{5,13},{6,14},{7,15},{8,0},{9,1},... | collective-permute-start | bytes 983048 | tf_op jit(solution)/shard_map/ppermute | solution.py:501
  17.6 10.5 %collective-permute-start = (f32[288,256]{1,0:T(8,128)}, f32[288,256]{1,0:T(8,128)S(1)}, u32[]{:S(2)}, u32[]{:S(2)}) collective-permute-start(f32[288,256]{1,0:T(8,128)} %get-tuple-element.19), channel_id=1, source_target_pairs={{0,1},{1,2},{2,3},{3,4},{4,5},{5,6},{6,7},{7,8},{8,9},{9,10},{10,1... | collective-permute-start | bytes 884744 | tf_op jit(solution)/shard_map/ppermute | solution.py:513
  24.1 12.6 %collective-permute-start.1 = (f32[288,256]{1,0:T(8,128)}, f32[288,256]{1,0:T(8,128)S(1)}, u32[]{:S(2)}, u32[]{:S(2)}) collective-permute-start(f32[288,256]{1,0:T(8,128)} %get-tuple-element.20), channel_id=1, source_target_pairs={{1,0},{2,1},{3,2},{4,3},{5,4},{6,5},{7,6},{8,7},{9,8},{10,9},{11,1... | collective-permute-start | bytes 884744 | tf_op jit(solution)/shard_map/ppermute | solution.py:513
  26.0 27.7 %collective-permute-start.3 = (f32[8,80,128]{2,1,0:T(8,128)S(1)}, f32[8,80,128]{2,1,0:T(8,128)S(1)}, u32[]{:S(2)}, u32[]{:S(2)}) collective-permute-start(f32[8,80,128]{2,1,0:T(8,128)S(1)} %all_to_all.10.rest_0_.rest_7_), channel_id=1, source_target_pairs={{0,32},{1,33},{2,34},{3,35},{4,36},{5,37},{6,38},{7,39},{8,40},{9,... | collective-permute-start | bytes 983048 | tf_op jit(solution)/shard_map/ppermute | solution.py:501
  26.4 27.3 %collective-permute-start.4 = (f32[8,80,128]{2,1,0:T(8,128)S(1)}, f32[8,80,128]{2,1,0:T(8,128)S(1)}, u32[]{:S(2)}, u32[]{:S(2)}) collective-permute-start(f32[8,80,128]{2,1,0:T(8,128)S(1)} %collective-permute-done.2.rest_1_.rest_8_), channel_id=1, source_target_pairs={{0,32},{1,33},{2,34},{3,35},{4,36},{5,37},{6,38},{7,39},{8,40},{9,... | collective-permute-start | bytes 983048 | tf_op jit(solution)/shard_map/ppermute | solution.py:501
  57.4 3.2 %collective-permute-start.7 = (f32[32,128]{1,0:T(8,128)S(1)}, f32[32,128]{1,0:T(8,128)S(1)}, u32[]{:S(2)}, u32[]{:S(2)}) collective-permute-start(f32[32,128]{1,0:T(8,128)S(1)} %get-tuple-element.24.rest_0_), channel_id=1, source_target_pairs={{0,3},{1,2},{2,1},{3,0},{4,7},{5,6},{6,5},{7,4},{8,11},{9,10},{10,... | collective-permute-start | bytes 49160 | tf_op jit(solution)/shard_map/ppermute | solution.py:501
  58.4 2.9 %collective-permute-start.6 = (f32[32,128]{1,0:T(8,128)S(1)}, f32[32,128]{1,0:T(8,128)S(1)}, u32[]{:S(2)}, u32[]{:S(2)}) collective-permute-start(f32[32,128]{1,0:T(8,128)S(1)} %get-tuple-element.24.rest_0_), channel_id=1, source_target_pairs={{0,2},{1,3},{2,0},{3,1},{4,6},{5,7},{6,4},{7,5},{8,10},{9,11},{10,... | collective-permute-start | bytes 49160 | tf_op jit(solution)/shard_map/ppermute | solution.py:501
  59.8 1.4 %collective-permute-start.5 = (f32[32,128]{1,0:T(8,128)S(1)}, f32[32,128]{1,0:T(8,128)S(1)}, u32[]{:S(2)}, u32[]{:S(2)}) collective-permute-start(f32[32,128]{1,0:T(8,128)S(1)} %get-tuple-element.24.rest_0_), channel_id=1, source_target_pairs={{0,1},{1,0},{2,3},{3,2},{4,5},{5,4},{6,7},{7,6},{8,9},{9,8},{10,11... | collective-permute-start | bytes 49160 | tf_op jit(solution)/shard_map/ppermute | solution.py:501
  63.3 3.6 %collective-permute-start.10 = (f32[32,128]{1,0:T(8,128)S(1)}, f32[32,128]{1,0:T(8,128)S(1)}, u32[]{:S(2)}, u32[]{:S(2)}) collective-permute-start(f32[32,128]{1,0:T(8,128)S(1)} %shard_map.106.rest_0_), channel_id=1, source_target_pairs={{0,3},{1,2},{2,1},{3,0},{4,7},{5,6},{6,5},{7,4},{8,11},{9,10},{10,... | collective-permute-start | bytes 49160 | tf_op jit(solution)/shard_map/ppermute | solution.py:501
  65.3 3.1 %collective-permute-start.9 = (f32[32,128]{1,0:T(8,128)S(1)}, f32[32,128]{1,0:T(8,128)S(1)}, u32[]{:S(2)}, u32[]{:S(2)}) collective-permute-start(f32[32,128]{1,0:T(8,128)S(1)} %shard_map.106.rest_0_), channel_id=1, source_target_pairs={{0,2},{1,3},{2,0},{3,1},{4,6},{5,7},{6,4},{7,5},{8,10},{9,11},{10,... | collective-permute-start | bytes 49160 | tf_op jit(solution)/shard_map/ppermute | solution.py:501
  67.0 1.4 %collective-permute-start.8 = (f32[32,128]{1,0:T(8,128)S(1)}, f32[32,128]{1,0:T(8,128)S(1)}, u32[]{:S(2)}, u32[]{:S(2)}) collective-permute-start(f32[32,128]{1,0:T(8,128)S(1)} %shard_map.106.rest_0_), channel_id=1, source_target_pairs={{0,1},{1,0},{2,3},{3,2},{4,5},{5,4},{6,7},{7,6},{8,9},{9,8},{10,11... | collective-permute-start | bytes 49160 | tf_op jit(solution)/shard_map/ppermute | solution.py:501
  70.5 32.0 %copy-start.5 = (f32[8,128]{1,0:T(8,128)S(1)}, f32[8,128]{1,0:T(8,128)}, u32[]{:S(2)}) copy-start(f32[8,128]{1,0:T(8,128)} %get-tuple-element.31.rest_9_) | copy-start | bytes 12292
  70.5 3.4 %collective-permute-start.13 = (f32[32,128]{1,0:T(8,128)S(1)}, f32[32,128]{1,0:T(8,128)S(1)}, u32[]{:S(2)}, u32[]{:S(2)}) collective-permute-start(f32[32,128]{1,0:T(8,128)S(1)} %shard_map.107.rest_0_), channel_id=1, source_target_pairs={{0,3},{1,2},{2,1},{3,0},{4,7},{5,6},{6,5},{7,4},{8,11},{9,10},{10,... | collective-permute-start | bytes 49160 | tf_op jit(solution)/shard_map/ppermute | solution.py:501
  71.7 3.6 %collective-permute-start.12 = (f32[32,128]{1,0:T(8,128)S(1)}, f32[32,128]{1,0:T(8,128)S(1)}, u32[]{:S(2)}, u32[]{:S(2)}) collective-permute-start(f32[32,128]{1,0:T(8,128)S(1)} %shard_map.107.rest_0_), channel_id=1, source_target_pairs={{0,2},{1,3},{2,0},{3,1},{4,6},{5,7},{6,4},{7,5},{8,10},{9,11},{10,... | collective-permute-start | bytes 49160 | tf_op jit(solution)/shard_map/ppermute | solution.py:501
  73.9 1.4 %collective-permute-start.11 = (f32[32,128]{1,0:T(8,128)S(1)}, f32[32,128]{1,0:T(8,128)S(1)}, u32[]{:S(2)}, u32[]{:S(2)}) collective-permute-start(f32[32,128]{1,0:T(8,128)S(1)} %shard_map.107.rest_0_), channel_id=1, source_target_pairs={{0,1},{1,0},{2,3},{3,2},{4,5},{5,4},{6,7},{7,6},{8,9},{9,8},{10,11... | collective-permute-start | bytes 49160 | tf_op jit(solution)/shard_map/ppermute | solution.py:501
  77.4 3.2 %collective-permute-start.16 = (f32[32,128]{1,0:T(8,128)S(1)}, f32[32,128]{1,0:T(8,128)S(1)}, u32[]{:S(2)}, u32[]{:S(2)}) collective-permute-start(f32[32,128]{1,0:T(8,128)S(1)} %shard_map.108.rest_0_), channel_id=1, source_target_pairs={{0,3},{1,2},{2,1},{3,0},{4,7},{5,6},{6,5},{7,4},{8,11},{9,10},{10,... | collective-permute-start | bytes 49160 | tf_op jit(solution)/shard_map/ppermute | solution.py:501
  78.4 3.6 %collective-permute-start.15 = (f32[32,128]{1,0:T(8,128)S(1)}, f32[32,128]{1,0:T(8,128)S(1)}, u32[]{:S(2)}, u32[]{:S(2)}) collective-permute-start(f32[32,128]{1,0:T(8,128)S(1)} %shard_map.108.rest_0_), channel_id=1, source_target_pairs={{0,2},{1,3},{2,0},{3,1},{4,6},{5,7},{6,4},{7,5},{8,10},{9,11},{10,... | collective-permute-start | bytes 49160 | tf_op jit(solution)/shard_map/ppermute | solution.py:501
  80.6 1.4 %collective-permute-start.14 = (f32[32,128]{1,0:T(8,128)S(1)}, f32[32,128]{1,0:T(8,128)S(1)}, u32[]{:S(2)}, u32[]{:S(2)}) collective-permute-start(f32[32,128]{1,0:T(8,128)S(1)} %shard_map.108.rest_0_), channel_id=1, source_target_pairs={{0,1},{1,0},{2,3},{3,2},{4,5},{5,4},{6,7},{7,6},{8,9},{9,8},{10,11... | collective-permute-start | bytes 49160 | tf_op jit(solution)/shard_map/ppermute | solution.py:501
  84.1 18.3 %collective-permute-start.19 = (f32[32,128]{1,0:T(8,128)S(1)}, f32[32,128]{1,0:T(8,128)S(1)}, u32[]{:S(2)}, u32[]{:S(2)}) collective-permute-start(f32[32,128]{1,0:T(8,128)S(1)} %shard_map.109.rest_0_), channel_id=1, source_target_pairs={{0,3},{1,2},{2,1},{3,0},{4,7},{5,6},{6,5},{7,4},{8,11},{9,10},{10,... | collective-permute-start | bytes 49160 | tf_op jit(solution)/shard_map/ppermute | solution.py:501
  85.3 17.1 %collective-permute-start.18 = (f32[32,128]{1,0:T(8,128)S(1)}, f32[32,128]{1,0:T(8,128)S(1)}, u32[]{:S(2)}, u32[]{:S(2)}) collective-permute-start(f32[32,128]{1,0:T(8,128)S(1)} %shard_map.109.rest_0_), channel_id=1, source_target_pairs={{0,2},{1,3},{2,0},{3,1},{4,6},{5,7},{6,4},{7,5},{8,10},{9,11},{10,... | collective-permute-start | bytes 49160 | tf_op jit(solution)/shard_map/ppermute | solution.py:501
  87.5 15.0 %collective-permute-start.17 = (f32[32,128]{1,0:T(8,128)S(1)}, f32[32,128]{1,0:T(8,128)S(1)}, u32[]{:S(2)}, u32[]{:S(2)}) collective-permute-start(f32[32,128]{1,0:T(8,128)S(1)} %shard_map.109.rest_0_), channel_id=1, source_target_pairs={{0,1},{1,0},{2,3},{3,2},{4,5},{5,4},{6,7},{7,6},{8,9},{9,8},{10,11... | collective-permute-start | bytes 49160 | tf_op jit(solution)/shard_map/ppermute | solution.py:501
  87.5 7.7 %collective-permute-start.20 = (f32[3,256]{1,0:T(4,128)S(1)}, f32[3,256]{1,0:T(4,128)S(1)}, u32[]{:S(2)}, u32[]{:S(2)}) collective-permute-start(f32[3,256]{1,0:T(4,128)S(1)} %get-tuple-element.32), channel_id=1, source_target_pairs={{0,1},{1,2},{2,3},{3,4},{4,5},{5,6},{6,7},{7,8},{8,9},{9,10},{10,1... | collective-permute-start | bytes 9224 | tf_op jit(solution)/shard_map/ppermute | solution.py:513
  93.3 9.1 %collective-permute-start.21 = (f32[3,256]{1,0:T(4,128)S(1)}, f32[3,256]{1,0:T(4,128)S(1)}, u32[]{:S(2)}, u32[]{:S(2)}) collective-permute-start(f32[3,256]{1,0:T(4,128)S(1)} %get-tuple-element.33), channel_id=1, source_target_pairs={{1,0},{2,1},{3,2},{4,3},{5,4},{6,5},{7,6},{8,7},{9,8},{10,9},{11,1... | collective-permute-start | bytes 9224 | tf_op jit(solution)/shard_map/ppermute | solution.py:513

commit v3 on v0

--- a/solution.py
+++ b/solution.py
@@ -340,13 +340,13 @@
                 a = data[d // NEAR][d % NEAR, lanes8(3 * i), :] * near[0]
                 a = a + data[d // NEAR][d % NEAR, lanes8(3 * i + 1), :] * near[1]
                 a = a + data[d // NEAR][d % NEAR, lanes8(3 * i + 2), :] * near[2]
-                gather[i, d : d + 1, :] += jnp.sum(a, axis=0, keepdims=True)
+                gather[i, d] += a
         return carry
 
     lax.fori_loop(0, passes, one_pass, 0)
     parts = []
     for i in range(3):
-        s = gather[i]
+        s = jnp.sum(gather[i], axis=1)
         s = s + pltpu.roll(s, 64, axis=1)
         parts.append(s + pltpu.roll(s, 32, axis=1))
     return own + damping * (rhs - (dia * own - spread(parts))) / dia
@@ -557,7 +557,7 @@
     before2, after2 = shifts(up2, down2)
     sums = lax.all_to_all(send, DOM, 0, 0, tiled=True)
     peers = ((PEERS, LANES), f32)
-    gather = (3, PEERS, LANES)
+    gather = (3, PEERS, 8, LANES)
     square = (LANES, LANES)
     new, crhs, cd, where, passes = call(
         coarse_first_kernel,

time: 105 us -> 106 us (level)
  transfers between devices with their start and end apart: 22 -> 22, of which waited for: 8 -> 9; matrix products, arithmetic and copies ran while one was open for 0% -> 0% of each run, Pallas kernels for 2% -> 2%
where the time goes in v3:
time: 106 us; the launch traced here: 105 us
  starting transfers between devices  33.7 us (32%)
  blocking collectives  29.3 us (28%)
  waiting for transfers between devices  22 us (21%)
  Pallas kernels  19.6 us (18%)
    ppermute x18, starting transfers between devices, partner(): lax.ppermute(value, DOM, [(i, i ^ bits) for i in range(lax.axis_size(DOM))])  17.6 us
    pallas_call x7, Pallas kernels, call(): pl.pallas_call(kernel, in_specs=[smem] * scalars + [vmem] * (len(args) -...  17.1 us
    ppermute x4, waiting for transfers between devices, shifts(): return (lax.ppermute(up, DOM, forward), lax.ppermute(down, DOM, backward))  16.3 us
    ppermute x4, starting transfers between devices, shifts(): return (lax.ppermute(up, DOM, forward), lax.ppermute(down, DOM, backward))  16.1 us
    all_to_all x1, blocking collectives, cycle(): sums = lax.all_to_all(send, DOM, 0, 0, tiled=True)  14.9 us
    all_to_all x1, blocking collectives, cycle(): lax.all_to_all(dsend, DOM, 0, 0, axis_index_groups=row_groups(), tiled=True)  14.5 us
    ppermute x18, waiting for transfers between devices, partner(): lax.ppermute(value, DOM, [(i, i ^ bits) for i in range(lax.axis_size(DOM))])  5.68 us
    pallas_call x1, Pallas kernels, cycle(): pl.pallas_call(pack_kernel, name='pack', in_specs=[far] * 8, out_specs=[v...  2.47 us
  transfers between devices with their start and end apart: 22, of which 9 were waited for; matrix products, arithmetic and copies ran while one was open for 0% of the time, Pallas kernels for 2%

profile of v3, /device:TPU:103, one launch (start us, length us, event | category | flops | bytes accessed | tf_op | source)
XLA Modules:
  0.0 105.5 jit_solution(7365541996918370542)
XLA Ops:
  0.7 2.5 %pack.1 = (f32[288,256]{1,0:T(8,128)}, f32[288,256]{1,0:T(8,128)}, f32[8,128]{1,0:T(8,128)}, f32[8,80,128]{2,1,0:T(8,128)}) custom-call(f32[3,1024]{1,0:T(4,128)} %bitcast.17, f32[3,1024]{1,0:T(4,128)} %bitcast.19, s32[27,1024]{1,0:T(8,128)} %bitcast.14, f32[3,3,27,1024]{3,2,1,0:T(8,128)} %bitcast.11, s32[8,128]{1,0:T(8,128)} %bitcast.21, s32[1,32]{1,0:T(1,128)} %bitcast.24, ...), custom_call_target="tpu_custom_call" | custom-call | tf_op jit(solution)/shard_map/pack/pallas_call | solution.py:528
  3.2 14.5 %all_to_all.10.rest_0_.rest_7_ = f32[8,80,128]{2,1,0:T(8,128)S(1)} all-to-all(f32[8,80,128]{2,1,0:T(8,128)} %get-tuple-element.22), channel_id=1, replica_groups={{0,6,24,30,96,102,120,126},{1,7,25,31,97,103,121,127},{2,4,26,28,98,100..., dimensions={0} | all-to-all | bytes 655360 | tf_op jit(solution)/shard_map/all_to_all | solution.py:544
  17.6 0.0 collective-permute-start.2
  17.6 6.5 %collective-permute-start = (f32[288,256]{1,0:T(8,128)}, f32[288,256]{1,0:T(8,128)S(1)}, u32[]{:S(2)}, u32[]{:S(2)}) collective-permute-start(f32[288,256]{1,0:T(8,128)} %get-tuple-element.19), channel_id=1, source_target_pairs={{0,1},{1,2},{2,3},{3,4},{4,5},{5,6},{6,7},{7,8},{8,9},{9,10},{10,1... | collective-permute-start | bytes 884744 | tf_op jit(solution)/shard_map/ppermute | solution.py:513
  24.1 1.9 %collective-permute-start.1 = (f32[288,256]{1,0:T(8,128)}, f32[288,256]{1,0:T(8,128)S(1)}, u32[]{:S(2)}, u32[]{:S(2)}) collective-permute-start(f32[288,256]{1,0:T(8,128)} %get-tuple-element.20), channel_id=1, source_target_pairs={{1,0},{2,1},{3,2},{4,3},{5,4},{6,5},{7,6},{8,7},{9,8},{10,9},{11,1... | collective-permute-start | bytes 884744 | tf_op jit(solution)/shard_map/ppermute | solution.py:513
  26.0 0.4 collective-permute-start.3
  26.4 0.0 collective-permute-done.2.rest_1_.rest_8_
  26.4 1.2 %collective-permute-start.4 = (f32[8,80,128]{2,1,0:T(8,128)S(1)}, f32[8,80,128]{2,1,0:T(8,128)S(1)}, u32[]{:S(2)}, u32[]{:S(2)}) collective-permute-start(f32[8,80,128]{2,1,0:T(8,128)S(1)} %collective-permute-done.2.rest_1_.rest_8_), channel_id=1, source_target_pairs={{0,32},{1,33},{2,34},{3,35},{4,36},{5,37},{6,38},{7,39},{8,40},{9,... | collective-permute-start | bytes 983048 | tf_op jit(solution)/shard_map/ppermute | solution.py:501
  27.6 0.5 collective-permute-done.before.rest_10_
  28.1 8.6 %collective-permute-done.1.after.rest_11_ = f32[288,256]{1,0:T(8,128)S(1)} collective-permute-done((f32[288,256]{1,0:T(8,128)}, f32[288,256]{1,0:T(8,128)S(1)}, u32[]{:S(2)}, u32[]{:S(2)}) %collective-permute-start.1) | collective-permute-done | bytes 294944 | tf_op jit(solution)/shard_map/ppermute | solution.py:513
  36.7 2.1 %shard_map.104 = (f32[128,2,128]{2,1,0:T(2,128)S(1)}, f32[3,2048]{1,0:T(4,128)S(1)}, f32[3,2048]{1,0:T(4,128)S(1)}, f32[3,2048]{1,0:T(4,128)S(1)}, f32[3,256]{1,0:T(4,128)S(1)}, /*index=5*/f32[3,256]{1,0:T(4,128)S(1)}) custom-call(s32[1]{0:T(128)} %bitcast.base_ref, f32[3,1024]{1,0:T(4,128)S(1)} %bitcast.18, f32[3,1024]{1,0:T(4,128)S(1)} %bitcast.20, ...), custom_call_target="tpu_custom_call" | custom-call | tf_op jit(solution)/shard_map/pallas_call | solution.py:488
  38.9 14.9 %all_to_all.11.sums = f32[128,2,128]{2,1,0:T(2,128)S(1)} all-to-all(f32[128,2,128]{2,1,0:T(2,128)S(1)} %get-tuple-element.21), channel_id=1, replica_groups=mesh['dom'=128] {'dom'}, dimensions={0} | all-to-all | bytes 262144 | tf_op jit(solution)/shard_map/all_to_all | solution.py:558
  53.7 0.0 collective-permute-done.3.rest_2_.rest_9_
  53.7 0.0 collective-permute-done.4.rest_3_.rest_10_
  53.7 3.7 %shard_map.105 = (f32[32,128]{1,0:T(8,128)S(1)}, f32[32,128]{1,0:T(8,128)S(1)}, f32[32,128]{1,0:T(8,128)S(1)}, s32[32,8,128]{2,1,0:T(8,128)S(1)}, s32[8,128]{1,0:T(8,128)S(1)}) custom-call(s32[1]{0:T(128)} %bitcast.base_ref, f32[128,2,128]{2,1,0:T(2,128)S(1)} %all_to_all.11.sums, f32[8,80,128]{2,1,0:T(8,128)S(1)} %all_to_all.10.rest_0_.rest_7_, ...), custom_call_target="tpu_custom_call" | custom-call | tf_op jit(solution)/shard_map/pallas_call | solution.py:488
  57.5 1.0 collective-permute-start.7
  58.4 1.5 %collective-permute-start.6 = (f32[32,128]{1,0:T(8,128)S(1)}, f32[32,128]{1,0:T(8,128)S(1)}, u32[]{:S(2)}, u32[]{:S(2)}) collective-permute-start(f32[32,128]{1,0:T(8,128)S(1)} %get-tuple-element.24.rest_0_), channel_id=1, source_target_pairs={{0,2},{1,3},{2,0},{3,1},{4,6},{5,7},{6,4},{7,5},{8,10},{9,11},{10,... | collective-permute-start | bytes 49160 | tf_op jit(solution)/shard_map/ppermute | solution.py:501
  59.9 0.0 collective-permute-start.5
  59.9 0.8 collective-permute-done.7.rest_3_
  60.7 0.6 collective-permute-done.6.rest_2_
  61.3 0.0 collective-permute-done.5.rest_1_
  61.3 2.1 %shard_map.106.rest_0_ = f32[32,128]{1,0:T(8,128)S(1)} custom-call(s32[1]{0:T(128)} %bitcast.base_ref, s32[8,128]{1,0:T(8,128)S(1)} %get-tuple-element.23.passes, f32[32,128]{1,0:T(8,128)S(1)} %get-tuple-element.24.rest_0_, f32[32,128]{1,0:T(8,128)S(1)} %collective-permute-done.5.rest_1_, f32[32,128]{1,0:T(8,128)S(1)} %collective-permute-done.6.rest_2_, ...), custom_call_target="tpu_custom_call" | custom-call | tf_op jit(solution)/shard_map/pallas_call | solution.py:488
  63.4 2.0 %collective-permute-start.10 = (f32[32,128]{1,0:T(8,128)S(1)}, f32[32,128]{1,0:T(8,128)S(1)}, u32[]{:S(2)}, u32[]{:S(2)}) collective-permute-start(f32[32,128]{1,0:T(8,128)S(1)} %shard_map.106.rest_0_), channel_id=1, source_target_pairs={{0,3},{1,2},{2,1},{3,0},{4,7},{5,6},{6,5},{7,4},{8,11},{9,10},{10,... | collective-permute-start | bytes 49160 | tf_op jit(solution)/shard_map/ppermute | solution.py:501
  65.4 1.6 %collective-permute-start.9 = (f32[32,128]{1,0:T(8,128)S(1)}, f32[32,128]{1,0:T(8,128)S(1)}, u32[]{:S(2)}, u32[]{:S(2)}) collective-permute-start(f32[32,128]{1,0:T(8,128)S(1)} %shard_map.106.rest_0_), channel_id=1, source_target_pairs={{0,2},{1,3},{2,0},{3,1},{4,6},{5,7},{6,4},{7,5},{8,10},{9,11},{10,... | collective-permute-start | bytes 49160 | tf_op jit(solution)/shard_map/ppermute | solution.py:501
  67.0 0.0 collective-permute-start.8
  67.0 1.4 %collective-permute-done.9.rest_2_ = f32[32,128]{1,0:T(8,128)S(1)} collective-permute-done((f32[32,128]{1,0:T(8,128)S(1)}, f32[32,128]{1,0:T(8,128)S(1)}, u32[]{:S(2)}, u32[]{:S(2)}) %collective-permute-start.9) | collective-permute-done | bytes 16416 | tf_op jit(solution)/shard_map/ppermute | solution.py:501
  68.5 2.1 %shard_map.107.rest_0_ = f32[32,128]{1,0:T(8,128)S(1)} custom-call(s32[1]{0:T(128)} %bitcast.base_ref, s32[8,128]{1,0:T(8,128)S(1)} %get-tuple-element.23.passes, f32[32,128]{1,0:T(8,128)S(1)} %shard_map.106.rest_0_, f32[32,128]{1,0:T(8,128)S(1)} %collective-permute-done.8.rest_1_, f32[32,128]{1,0:T(8,128)S(1)} %collective-permute-done.9.rest_2_, ...), custom_call_target="tpu_custom_call" | custom-call | tf_op jit(solution)/shard_map/pallas_call | solution.py:488
  70.6 0.0 copy-start.5
  70.6 1.2 %collective-permute-start.13 = (f32[32,128]{1,0:T(8,128)S(1)}, f32[32,128]{1,0:T(8,128)S(1)}, u32[]{:S(2)}, u32[]{:S(2)}) collective-permute-start(f32[32,128]{1,0:T(8,128)S(1)} %shard_map.107.rest_0_), channel_id=1, source_target_pairs={{0,3},{1,2},{2,1},{3,0},{4,7},{5,6},{6,5},{7,4},{8,11},{9,10},{10,... | collective-permute-start | bytes 49160 | tf_op jit(solution)/shard_map/ppermute | solution.py:501
  71.8 2.2 %collective-permute-start.12 = (f32[32,128]{1,0:T(8,128)S(1)}, f32[32,128]{1,0:T(8,128)S(1)}, u32[]{:S(2)}, u32[]{:S(2)}) collective-permute-start(f32[32,128]{1,0:T(8,128)S(1)} %shard_map.107.rest_0_), channel_id=1, source_target_pairs={{0,2},{1,3},{2,0},{3,1},{4,6},{5,7},{6,4},{7,5},{8,10},{9,11},{10,... | collective-permute-start | bytes 49160 | tf_op jit(solution)/shard_map/ppermute | solution.py:501
  74.0 0.0 collective-permute-start.11
  74.0 1.4 %collective-permute-done.12.rest_2_ = f32[32,128]{1,0:T(8,128)S(1)} collective-permute-done((f32[32,128]{1,0:T(8,128)S(1)}, f32[32,128]{1,0:T(8,128)S(1)}, u32[]{:S(2)}, u32[]{:S(2)}) %collective-permute-start.12) | collective-permute-done | bytes 16416 | tf_op jit(solution)/shard_map/ppermute | solution.py:501
  75.4 2.1 %shard_map.108.rest_0_ = f32[32,128]{1,0:T(8,128)S(1)} custom-call(s32[1]{0:T(128)} %bitcast.base_ref, s32[8,128]{1,0:T(8,128)S(1)} %get-tuple-element.23.passes, f32[32,128]{1,0:T(8,128)S(1)} %shard_map.107.rest_0_, f32[32,128]{1,0:T(8,128)S(1)} %collective-permute-done.11.rest_1_, f32[32,128]{1,0:T(8,128)S(1)} %collective-permute-done.12.rest_2_, ...), custom_call_target="tpu_custom_call" | custom-call | tf_op jit(solution)/shard_map/pallas_call | solution.py:488
  77.5 1.0 collective-permute-start.16
  78.6 2.2 %collective-permute-start.15 = (f32[32,128]{1,0:T(8,128)S(1)}, f32[32,128]{1,0:T(8,128)S(1)}, u32[]{:S(2)}, u32[]{:S(2)}) collective-permute-start(f32[32,128]{1,0:T(8,128)S(1)} %shard_map.108.rest_0_), channel_id=1, source_target_pairs={{0,2},{1,3},{2,0},{3,1},{4,6},{5,7},{6,4},{7,5},{8,10},{9,11},{10,... | collective-permute-start | bytes 49160 | tf_op jit(solution)/shard_map/ppermute | solution.py:501
  80.7 0.0 collective-permute-start.14
  80.7 0.1 collective-permute-done.16.rest_3_
  80.8 1.4 %collective-permute-done.15.rest_2_ = f32[32,128]{1,0:T(8,128)S(1)} collective-permute-done((f32[32,128]{1,0:T(8,128)S(1)}, f32[32,128]{1,0:T(8,128)S(1)}, u32[]{:S(2)}, u32[]{:S(2)}) %collective-permute-start.15) | collective-permute-done | bytes 16416 | tf_op jit(solution)/shard_map/ppermute | solution.py:501
  82.1 0.0 collective-permute-done.14.rest_1_
  82.1 2.3 %shard_map.109.rest_0_ = f32[32,128]{1,0:T(8,128)S(1)} custom-call(s32[1]{0:T(128)} %bitcast.base_ref, s32[8,128]{1,0:T(8,128)S(1)} %get-tuple-element.23.passes, f32[32,128]{1,0:T(8,128)S(1)} %shard_map.108.rest_0_, f32[32,128]{1,0:T(8,128)S(1)} %collective-permute-done.14.rest_1_, f32[32,128]{1,0:T(8,128)S(1)} %collective-permute-done.15.rest_2_, ...), custom_call_target="tpu_custom_call" | custom-call | tf_op jit(solution)/shard_map/pallas_call | solution.py:488
  84.4 1.2 %collective-permute-start.19 = (f32[32,128]{1,0:T(8,128)S(1)}, f32[32,128]{1,0:T(8,128)S(1)}, u32[]{:S(2)}, u32[]{:S(2)}) collective-permute-start(f32[32,128]{1,0:T(8,128)S(1)} %shard_map.109.rest_0_), channel_id=1, source_target_pairs={{0,3},{1,2},{2,1},{3,0},{4,7},{5,6},{6,5},{7,4},{8,11},{9,10},{10,... | collective-permute-start | bytes 49160 | tf_op jit(solution)/shard_map/ppermute | solution.py:501
  85.7 2.2 %collective-permute-start.18 = (f32[32,128]{1,0:T(8,128)S(1)}, f32[32,128]{1,0:T(8,128)S(1)}, u32[]{:S(2)}, u32[]{:S(2)}) collective-permute-start(f32[32,128]{1,0:T(8,128)S(1)} %shard_map.109.rest_0_), channel_id=1, source_target_pairs={{0,2},{1,3},{2,0},{3,1},{4,6},{5,7},{6,4},{7,5},{8,10},{9,11},{10,... | collective-permute-start | bytes 49160 | tf_op jit(solution)/shard_map/ppermute | solution.py:501
  87.9 0.0 collective-permute-start.17
  87.9 5.8 %collective-permute-start.20 = (f32[3,256]{1,0:T(4,128)S(1)}, f32[3,256]{1,0:T(4,128)S(1)}, u32[]{:S(2)}, u32[]{:S(2)}) collective-permute-start(f32[3,256]{1,0:T(4,128)S(1)} %get-tuple-element.32), channel_id=1, source_target_pairs={{0,1},{1,2},{2,3},{3,4},{4,5},{5,6},{6,7},{7,8},{8,9},{9,10},{10,1... | collective-permute-start | bytes 9224 | tf_op jit(solution)/shard_map/ppermute | solution.py:513
  93.6 1.9 %collective-permute-start.21 = (f32[3,256]{1,0:T(4,128)S(1)}, f32[3,256]{1,0:T(4,128)S(1)}, u32[]{:S(2)}, u32[]{:S(2)}) collective-permute-start(f32[3,256]{1,0:T(4,128)S(1)} %get-tuple-element.33), channel_id=1, source_target_pairs={{1,0},{2,1},{3,2},{4,3},{5,4},{6,5},{7,6},{8,7},{9,8},{10,9},{11,1... | collective-permute-start | bytes 9224 | tf_op jit(solution)/shard_map/ppermute | solution.py:513
  95.6 0.0 collective-permute-done.20.rest_12_
  95.6 7.2 %collective-permute-done.21.rest_13_ = f32[3,256]{1,0:T(4,128)S(1)} collective-permute-done((f32[3,256]{1,0:T(4,128)S(1)}, f32[3,256]{1,0:T(4,128)S(1)}, u32[]{:S(2)}, u32[]{:S(2)}) %collective-permute-start.21) | collective-permute-done | bytes 3104 | tf_op jit(solution)/shard_map/ppermute | solution.py:513
  102.8 2.7 %shard_map.110 = (f32[3,1024]{1,0:T(4,128)}, f32[3,32]{1,0:T(4,128)}) custom-call(s32[1]{0:T(128)} %bitcast.base_ref, f32[32,128]{1,0:T(8,128)S(1)} %shard_map.109.rest_0_, f32[32,128]{1,0:T(8,128)S(1)} %collective-permute-done.17.rest_1_, f32[32,128]{1,0:T(8,128)S(1)} %collective-permute-done.18.rest_2_, f32[32,128]{1,0:T(8,128)S(1)} %collective-permute-done.19.rest_3_, ...), custom_call_target="tpu_custom_call" | custom-call | tf_op jit(solution)/shard_map/pallas_call | solution.py:488
  (22 shorter events, 0.1 us)
Async XLA Ops:
  0.6 36.1 %copy-start.7 = (s32[32]{0:T(128)S(1)}, s32[32]{0:T(128)}, u32[]{:S(2)}) copy-start(s32[32]{0:T(128)} %param.14) | copy-start | bytes 388
  0.6 36.0 %copy-start.4 = (s32[1024]{0:T(1024)S(1)}, s32[1024]{0:T(1024)}, u32[]{:S(2)}) copy-start(s32[1024]{0:T(1024)} %param.13) | copy-start | bytes 12292
  0.7 36.0 %copy-start = (f32[1024,27,3,3]{0,1,3,2:T(8,128)S(1)}, f32[1024,27,3,3]{0,1,3,2:T(8,128)}, u32[]{:S(2)}) copy-start(f32[1024,27,3,3]{0,1,3,2:T(8,128)} %param.12) | copy-start | bytes 2985988
  0.7 36.0 %copy-start.1 = (s32[1024,27]{0,1:T(8,128)S(1)}, s32[1024,27]{0,1:T(8,128)}, u32[]{:S(2)}) copy-start(s32[1024,27]{0,1:T(8,128)} %param.11) | copy-start | bytes 331780
  0.7 36.0 %copy-start.3 = (f32[1024,3]{0,1:T(4,128)S(1)}, f32[1024,3]{0,1:T(4,128)}, u32[]{:S(2)}) copy-start(f32[1024,3]{0,1:T(4,128)} %param.10) | copy-start | bytes 36868
  0.7 36.0 %copy-start.2 = (f32[1024,3]{0,1:T(4,128)S(1)}, f32[1024,3]{0,1:T(4,128)}, u32[]{:S(2)}) copy-start(f32[1024,3]{0,1:T(4,128)} %param.9) | copy-start | bytes 36868
  0.7 36.0 %copy-start.6 = (f32[32,3]{0,1:T(4,128)S(1)}, f32[32,3]{0,1:T(4,128)}, u32[]{:S(2)}) copy-start(f32[32,3]{0,1:T(4,128)} %param.15) | copy-start | bytes 1156
  17.6 8.8 %collective-permute-start.2 = (f32[8,80,128]{2,1,0:T(8,128)S(1)}, f32[8,80,128]{2,1,0:T(8,128)S(1)}, u32[]{:S(2)}, u32[]{:S(2)}) collective-permute-start(f32[8,80,128]{2,1,0:T(8,128)S(1)} %all_to_all.10.rest_0_.rest_7_), channel_id=1, source_target_pairs={{0,8},{1,9},{2,10},{3,11},{4,12},{5,13},{6,14},{7,15},{8,0},{9,1},... | collective-permute-start | bytes 983048 | tf_op jit(solution)/shard_map/ppermute | solution.py:501
  17.6 10.5 %collective-permute-start = (f32[288,256]{1,0:T(8,128)}, f32[288,256]{1,0:T(8,128)S(1)}, u32[]{:S(2)}, u32[]{:S(2)}) collective-permute-start(f32[288,256]{1,0:T(8,128)} %get-tuple-element.19), channel_id=1, source_target_pairs={{0,1},{1,2},{2,3},{3,4},{4,5},{5,6},{6,7},{7,8},{8,9},{9,10},{10,1... | collective-permute-start | bytes 884744 | tf_op jit(solution)/shard_map/ppermute | solution.py:513
  24.1 12.6 %collective-permute-start.1 = (f32[288,256]{1,0:T(8,128)}, f32[288,256]{1,0:T(8,128)S(1)}, u32[]{:S(2)}, u32[]{:S(2)}) collective-permute-start(f32[288,256]{1,0:T(8,128)} %get-tuple-element.20), channel_id=1, source_target_pairs={{1,0},{2,1},{3,2},{4,3},{5,4},{6,5},{7,6},{8,7},{9,8},{10,9},{11,1... | collective-permute-start | bytes 884744 | tf_op jit(solution)/shard_map/ppermute | solution.py:513
  26.0 27.7 %collective-permute-start.3 = (f32[8,80,128]{2,1,0:T(8,128)S(1)}, f32[8,80,128]{2,1,0:T(8,128)S(1)}, u32[]{:S(2)}, u32[]{:S(2)}) collective-permute-start(f32[8,80,128]{2,1,0:T(8,128)S(1)} %all_to_all.10.rest_0_.rest_7_), channel_id=1, source_target_pairs={{0,32},{1,33},{2,34},{3,35},{4,36},{5,37},{6,38},{7,39},{8,40},{9,... | collective-permute-start | bytes 983048 | tf_op jit(solution)/shard_map/ppermute | solution.py:501
  26.4 27.3 %collective-permute-start.4 = (f32[8,80,128]{2,1,0:T(8,128)S(1)}, f32[8,80,128]{2,1,0:T(8,128)S(1)}, u32[]{:S(2)}, u32[]{:S(2)}) collective-permute-start(f32[8,80,128]{2,1,0:T(8,128)S(1)} %collective-permute-done.2.rest_1_.rest_8_), channel_id=1, source_target_pairs={{0,32},{1,33},{2,34},{3,35},{4,36},{5,37},{6,38},{7,39},{8,40},{9,... | collective-permute-start | bytes 983048 | tf_op jit(solution)/shard_map/ppermute | solution.py:501
  57.5 3.2 %collective-permute-start.7 = (f32[32,128]{1,0:T(8,128)S(1)}, f32[32,128]{1,0:T(8,128)S(1)}, u32[]{:S(2)}, u32[]{:S(2)}) collective-permute-start(f32[32,128]{1,0:T(8,128)S(1)} %get-tuple-element.24.rest_0_), channel_id=1, source_target_pairs={{0,3},{1,2},{2,1},{3,0},{4,7},{5,6},{6,5},{7,4},{8,11},{9,10},{10,... | collective-permute-start | bytes 49160 | tf_op jit(solution)/shard_map/ppermute | solution.py:501
  58.4 2.9 %collective-permute-start.6 = (f32[32,128]{1,0:T(8,128)S(1)}, f32[32,128]{1,0:T(8,128)S(1)}, u32[]{:S(2)}, u32[]{:S(2)}) collective-permute-start(f32[32,128]{1,0:T(8,128)S(1)} %get-tuple-element.24.rest_0_), channel_id=1, source_target_pairs={{0,2},{1,3},{2,0},{3,1},{4,6},{5,7},{6,4},{7,5},{8,10},{9,11},{10,... | collective-permute-start | bytes 49160 | tf_op jit(solution)/shard_map/ppermute | solution.py:501
  59.9 1.4 %collective-permute-start.5 = (f32[32,128]{1,0:T(8,128)S(1)}, f32[32,128]{1,0:T(8,128)S(1)}, u32[]{:S(2)}, u32[]{:S(2)}) collective-permute-start(f32[32,128]{1,0:T(8,128)S(1)} %get-tuple-element.24.rest_0_), channel_id=1, source_target_pairs={{0,1},{1,0},{2,3},{3,2},{4,5},{5,4},{6,7},{7,6},{8,9},{9,8},{10,11... | collective-permute-start | bytes 49160 | tf_op jit(solution)/shard_map/ppermute | solution.py:501
  63.4 3.6 %collective-permute-start.10 = (f32[32,128]{1,0:T(8,128)S(1)}, f32[32,128]{1,0:T(8,128)S(1)}, u32[]{:S(2)}, u32[]{:S(2)}) collective-permute-start(f32[32,128]{1,0:T(8,128)S(1)} %shard_map.106.rest_0_), channel_id=1, source_target_pairs={{0,3},{1,2},{2,1},{3,0},{4,7},{5,6},{6,5},{7,4},{8,11},{9,10},{10,... | collective-permute-start | bytes 49160 | tf_op jit(solution)/shard_map/ppermute | solution.py:501
  65.4 3.1 %collective-permute-start.9 = (f32[32,128]{1,0:T(8,128)S(1)}, f32[32,128]{1,0:T(8,128)S(1)}, u32[]{:S(2)}, u32[]{:S(2)}) collective-permute-start(f32[32,128]{1,0:T(8,128)S(1)} %shard_map.106.rest_0_), channel_id=1, source_target_pairs={{0,2},{1,3},{2,0},{3,1},{4,6},{5,7},{6,4},{7,5},{8,10},{9,11},{10,... | collective-permute-start | bytes 49160 | tf_op jit(solution)/shard_map/ppermute | solution.py:501
  67.0 1.4 %collective-permute-start.8 = (f32[32,128]{1,0:T(8,128)S(1)}, f32[32,128]{1,0:T(8,128)S(1)}, u32[]{:S(2)}, u32[]{:S(2)}) collective-permute-start(f32[32,128]{1,0:T(8,128)S(1)} %shard_map.106.rest_0_), channel_id=1, source_target_pairs={{0,1},{1,0},{2,3},{3,2},{4,5},{5,4},{6,7},{7,6},{8,9},{9,8},{10,11... | collective-permute-start | bytes 49160 | tf_op jit(solution)/shard_map/ppermute | solution.py:501
  70.6 32.2 %copy-start.5 = (f32[8,128]{1,0:T(8,128)S(1)}, f32[8,128]{1,0:T(8,128)}, u32[]{:S(2)}) copy-start(f32[8,128]{1,0:T(8,128)} %get-tuple-element.31.rest_9_) | copy-start | bytes 12292
  70.6 3.4 %collective-permute-start.13 = (f32[32,128]{1,0:T(8,128)S(1)}, f32[32,128]{1,0:T(8,128)S(1)}, u32[]{:S(2)}, u32[]{:S(2)}) collective-permute-start(f32[32,128]{1,0:T(8,128)S(1)} %shard_map.107.rest_0_), channel_id=1, source_target_pairs={{0,3},{1,2},{2,1},{3,0},{4,7},{5,6},{6,5},{7,4},{8,11},{9,10},{10,... | collective-permute-start | bytes 49160 | tf_op jit(solution)/shard_map/ppermute | solution.py:501
  71.8 3.6 %collective-permute-start.12 = (f32[32,128]{1,0:T(8,128)S(1)}, f32[32,128]{1,0:T(8,128)S(1)}, u32[]{:S(2)}, u32[]{:S(2)}) collective-permute-start(f32[32,128]{1,0:T(8,128)S(1)} %shard_map.107.rest_0_), channel_id=1, source_target_pairs={{0,2},{1,3},{2,0},{3,1},{4,6},{5,7},{6,4},{7,5},{8,10},{9,11},{10,... | collective-permute-start | bytes 49160 | tf_op jit(solution)/shard_map/ppermute | solution.py:501
  74.0 1.4 %collective-permute-start.11 = (f32[32,128]{1,0:T(8,128)S(1)}, f32[32,128]{1,0:T(8,128)S(1)}, u32[]{:S(2)}, u32[]{:S(2)}) collective-permute-start(f32[32,128]{1,0:T(8,128)S(1)} %shard_map.107.rest_0_), channel_id=1, source_target_pairs={{0,1},{1,0},{2,3},{3,2},{4,5},{5,4},{6,7},{7,6},{8,9},{9,8},{10,11... | collective-permute-start | bytes 49160 | tf_op jit(solution)/shard_map/ppermute | solution.py:501
  77.5 3.2 %collective-permute-start.16 = (f32[32,128]{1,0:T(8,128)S(1)}, f32[32,128]{1,0:T(8,128)S(1)}, u32[]{:S(2)}, u32[]{:S(2)}) collective-permute-start(f32[32,128]{1,0:T(8,128)S(1)} %shard_map.108.rest_0_), channel_id=1, source_target_pairs={{0,3},{1,2},{2,1},{3,0},{4,7},{5,6},{6,5},{7,4},{8,11},{9,10},{10,... | collective-permute-start | bytes 49160 | tf_op jit(solution)/shard_map/ppermute | solution.py:501
  78.6 3.6 %collective-permute-start.15 = (f32[32,128]{1,0:T(8,128)S(1)}, f32[32,128]{1,0:T(8,128)S(1)}, u32[]{:S(2)}, u32[]{:S(2)}) collective-permute-start(f32[32,128]{1,0:T(8,128)S(1)} %shard_map.108.rest_0_), channel_id=1, source_target_pairs={{0,2},{1,3},{2,0},{3,1},{4,6},{5,7},{6,4},{7,5},{8,10},{9,11},{10,... | collective-permute-start | bytes 49160 | tf_op jit(solution)/shard_map/ppermute | solution.py:501
  80.7 1.4 %collective-permute-start.14 = (f32[32,128]{1,0:T(8,128)S(1)}, f32[32,128]{1,0:T(8,128)S(1)}, u32[]{:S(2)}, u32[]{:S(2)}) collective-permute-start(f32[32,128]{1,0:T(8,128)S(1)} %shard_map.108.rest_0_), channel_id=1, source_target_pairs={{0,1},{1,0},{2,3},{3,2},{4,5},{5,4},{6,7},{7,6},{8,9},{9,8},{10,11... | collective-permute-start | bytes 49160 | tf_op jit(solution)/shard_map/ppermute | solution.py:501
  84.4 18.3 %collective-permute-start.19 = (f32[32,128]{1,0:T(8,128)S(1)}, f32[32,128]{1,0:T(8,128)S(1)}, u32[]{:S(2)}, u32[]{:S(2)}) collective-permute-start(f32[32,128]{1,0:T(8,128)S(1)} %shard_map.109.rest_0_), channel_id=1, source_target_pairs={{0,3},{1,2},{2,1},{3,0},{4,7},{5,6},{6,5},{7,4},{8,11},{9,10},{10,... | collective-permute-start | bytes 49160 | tf_op jit(solution)/shard_map/ppermute | solution.py:501
  85.7 17.1 %collective-permute-start.18 = (f32[32,128]{1,0:T(8,128)S(1)}, f32[32,128]{1,0:T(8,128)S(1)}, u32[]{:S(2)}, u32[]{:S(2)}) collective-permute-start(f32[32,128]{1,0:T(8,128)S(1)} %shard_map.109.rest_0_), channel_id=1, source_target_pairs={{0,2},{1,3},{2,0},{3,1},{4,6},{5,7},{6,4},{7,5},{8,10},{9,11},{10,... | collective-permute-start | bytes 49160 | tf_op jit(solution)/shard_map/ppermute | solution.py:501
  87.9 14.9 %collective-permute-start.17 = (f32[32,128]{1,0:T(8,128)S(1)}, f32[32,128]{1,0:T(8,128)S(1)}, u32[]{:S(2)}, u32[]{:S(2)}) collective-permute-start(f32[32,128]{1,0:T(8,128)S(1)} %shard_map.109.rest_0_), channel_id=1, source_target_pairs={{0,1},{1,0},{2,3},{3,2},{4,5},{5,4},{6,7},{7,6},{8,9},{9,8},{10,11... | collective-permute-start | bytes 49160 | tf_op jit(solution)/shard_map/ppermute | solution.py:501
  87.9 7.7 %collective-permute-start.20 = (f32[3,256]{1,0:T(4,128)S(1)}, f32[3,256]{1,0:T(4,128)S(1)}, u32[]{:S(2)}, u32[]{:S(2)}) collective-permute-start(f32[3,256]{1,0:T(4,128)S(1)} %get-tuple-element.32), channel_id=1, source_target_pairs={{0,1},{1,2},{2,3},{3,4},{4,5},{5,6},{6,7},{7,8},{8,9},{9,10},{10,1... | collective-permute-start | bytes 9224 | tf_op jit(solution)/shard_map/ppermute | solution.py:513
  93.6 9.1 %collective-permute-start.21 = (f32[3,256]{1,0:T(4,128)S(1)}, f32[3,256]{1,0:T(4,128)S(1)}, u32[]{:S(2)}, u32[]{:S(2)}) collective-permute-start(f32[3,256]{1,0:T(4,128)S(1)} %get-tuple-element.33), channel_id=1, source_target_pairs={{1,0},{2,1},{3,2},{4,3},{5,4},{6,5},{7,6},{8,7},{9,8},{10,9},{11,1... | collective-permute-start | bytes 9224 | tf_op jit(solution)/shard_map/ppermute | solution.py:513
